TPU v7x, 256 devices: a whole 4x4x8 slice. The times are simulated.
256 devices in a mesh: seq: 32 (over y, z), head: 8 (over x, core).
Axes of the slice: x: 4, y: 4, z: 8, core: 2. Of those that a mesh axis runs over, the one named last changes fastest.
Arguments:
- tokens: bfloat16 [24576, 2560], P(('seq', 'head')), may hold values from -12 to 12
- pre_gain: float32 [2560], replicated, may hold values from 0.25 to 1.75
- inner_proj: bfloat16 [2560, 2, 5120], P(None, None, 'head'), may hold values from -0.125 to 0.125
- outer_proj: bfloat16 [2560, 336], replicated, may hold values from -0.125 to 0.125
- kernel_x: float32 [4, 5120], P(None, 'head'), may hold values from -3 to 3
- kernel_bc: float32 [4, 256], replicated, may hold values from -3 to 3
- offset_x: float32 [5120], P('head'), may hold values from -3 to 3
- offset_bc: float32 [256], replicated, may hold values from -3 to 3
- dt_bias: float32 [80], P('head'), may hold values from -7 to -5
- a_log: float32 [80], P('head'), may hold values from -12 to 4
- skip_gain: float32 [80], P('head'), may hold values from 0.5 to 1.5
- norm_gain: float32 [5120], P('head'), may hold values from 0.25 to 1.75
- out_proj: bfloat16 [5120, 2560], P('head'), may hold values from -0.078125 to 0.078125
Outputs:
- mixed: bfloat16 [24576, 2560], P(('seq', 'head'))
All inputs are finite; a program needn't handle non-finite values.
Results may differ from a plain program's by a relative error of at most 0.014.
Values may be sent and summed in bfloat16 or wider, within the bound.
A program may use at most 128 MiB of HBM per device.

v0:
```python
import jax
import jax.numpy as jnp
from jax import lax
from jax.sharding import Mesh
from jax.sharding import PartitionSpec as P

SPAN = 256
SEQ = ("seq_0", "seq_1")
SEQ_HEAD = ("seq_0", "seq_1", "head")


norm_floor = 0.1


def passed_along(block, axis, distance):
    devices = range(lax.axis_size(axis))
    route = [(i - distance, i) for i in devices if i - distance in devices]
    return lax.ppermute(block, axis, route)


def nothing_yet(array, identity):
    return jax.tree.map(
        lambda part, zero: jnp.zeros_like(part) + jnp.asarray(zero, part.dtype), array, identity
    )


def entering(array, axes, combine, identity):
    before = start = nothing_yet(array, identity)
    subtotal = array
    for axis in reversed(axes):
        length, position = (lax.axis_size(axis), lax.axis_index(axis))
        pieces = jax.tree.map(
            lambda part, kind: lax.all_gather(part.astype(kind), axis),
            subtotal,
            (jnp.bfloat16, jnp.bfloat16),
        )
        inside, subtotal = (start, start)
        for k in range(length):
            passed = k < position
            subtotal = combine(
                subtotal, jax.tree.map(lambda part, own: part[k].astype(own.dtype), pieces, array)
            )
            inside = jax.tree.map(lambda new, old: jnp.where(passed, new, old), subtotal, inside)
        before = combine(inside, before)
    return before


def from_everyone(array, axis):
    length = lax.axis_size(axis)
    return lax.all_to_all(
        jnp.broadcast_to(array[None], (length, *array.shape)), axis, 0, 0, tiled=True
    )


def taken_together(array, axis):
    everything = from_everyone(array, axis)
    return jnp.sum(everything, axis=0)


def cut_along(array, dim, length):
    before, after = (array.shape[:dim], array.shape[dim + 1 :])
    return jnp.moveaxis(array.reshape(*before, length, -1, *after), dim, 0)


def summed_on_arrival(array, axis, dim):
    pieces = cut_along(array, dim, lax.axis_size(axis))
    arrived = lax.all_to_all(pieces, axis, split_axis=0, concat_axis=0, tiled=True)
    return arrived.astype(jnp.float32).sum(axis=0)


def row_norm(row_block, gain_vector):
    widened = row_block.astype(jnp.float32)
    inverse_rms = lax.rsqrt(jnp.mean(widened * widened, axis=-1, keepdims=True) + norm_floor)
    return widened * inverse_rms * gain_vector


def masked_exp(log_gap, causal):
    return jnp.where(causal, jnp.exp(jnp.where(causal, log_gap, 0.0)), 0.0)


def on_device(
    tokens,
    pre_gain,
    inner_proj,
    outer_proj,
    kernel_x,
    kernel_bc,
    offset_x,
    offset_bc,
    dt_bias,
    a_log,
    skip_gain,
    norm_gain,
    out_proj,
):
    model_width = inner_proj.shape[0]
    local_width = inner_proj.shape[2]
    head_count = dt_bias.shape[0]
    head_size = local_width // head_count
    state_size = kernel_bc.shape[1] // 2
    kernel_size = kernel_x.shape[0]
    joined_proj = inner_proj.reshape(model_width, 2 * local_width)
    own_normed = row_norm(tokens, pre_gain).astype(jnp.bfloat16)
    normed = lax.all_gather(own_normed, "head", axis=0, tiled=True)
    inner_part = jnp.dot(normed, joined_proj, preferred_element_type=jnp.float32)
    outer_part = jnp.dot(normed, outer_proj, preferred_element_type=jnp.float32)
    projected = jnp.concatenate([inner_part, outer_part], axis=1)
    seq_rows = projected.shape[0]
    gate_in = projected[:, :local_width].astype(jnp.bfloat16)
    conv_input = projected[:, local_width : 2 * local_width + 2 * state_size].astype(jnp.bfloat16)
    head_index = lax.axis_index("head")
    dt_raw = lax.dynamic_slice_in_dim(
        projected[:, 2 * local_width + 2 * state_size :], head_index * head_count, head_count, 1
    )
    conv_tail = passed_along(conv_input[seq_rows - kernel_size + 1 :], SEQ, 1)
    extended = jnp.concatenate([conv_tail, conv_input], axis=0)
    conv_weight = jnp.concatenate([kernel_x, kernel_bc], axis=1)
    conv_bias = jnp.concatenate([offset_x, offset_bc])
    summed = jnp.broadcast_to(conv_bias, conv_input.shape)
    for offset in range(kernel_size):
        summed = summed + conv_weight[offset] * extended[offset : offset + seq_rows].astype(
            jnp.float32
        )
    conv_out = jax.nn.silu(summed).astype(jnp.bfloat16)
    blocks = seq_rows // SPAN
    values_x = conv_out[:, :local_width].reshape(blocks, SPAN, head_count, head_size)
    values_b = conv_out[:, local_width : local_width + state_size].reshape(blocks, SPAN, state_size)
    values_c = conv_out[:, local_width + state_size :].reshape(blocks, SPAN, state_size)
    step_flat = jax.nn.softplus(dt_raw + dt_bias)
    log_rates = (step_flat * -jnp.exp(a_log)).reshape(blocks, SPAN, head_count)
    step_sizes = step_flat.reshape(blocks, SPAN, head_count)
    running = jnp.cumsum(log_rates, axis=1)
    score_rows = jnp.einsum("ctn,csn->cts", values_c, values_b, preferred_element_type=jnp.float32)
    running_heads = jnp.transpose(running, (0, 2, 1))
    steps_heads = jnp.transpose(step_sizes, (0, 2, 1))
    row_index = lax.broadcasted_iota(jnp.int32, (SPAN, SPAN), 0)
    col_index = lax.broadcasted_iota(jnp.int32, (SPAN, SPAN), 1)
    decay_factor = masked_exp(
        running_heads[:, :, :, None] - running_heads[:, :, None, :], row_index >= col_index
    )
    mix_weights = (score_rows[:, None] * decay_factor * steps_heads[:, :, None, :]).astype(
        jnp.bfloat16
    )
    intra_out = jnp.einsum(
        "chts,cshp->cthp", mix_weights, values_x, preferred_element_type=jnp.float32
    )
    end_weight = jnp.exp(running[:, -1:, :] - running) * step_sizes
    scaled_x = (values_x.astype(jnp.float32) * end_weight[..., None]).astype(jnp.bfloat16)
    block_states = jnp.einsum(
        "cshp,csn->chpn", scaled_x, values_b, preferred_element_type=jnp.float32
    )
    block_total = running[:, -1, :]
    prefix_rate = jnp.concatenate(
        [jnp.zeros((1, head_count), jnp.float32), jnp.cumsum(block_total, axis=0)], axis=0
    )
    prefix_heads = prefix_rate.T
    later_index = lax.broadcasted_iota(jnp.int32, (blocks + 1, blocks), 0)
    source_index = lax.broadcasted_iota(jnp.int32, (blocks + 1, blocks), 1)
    link_weight = masked_exp(
        prefix_heads[:, :, None] - prefix_heads[:, None, 1:], source_index < later_index
    )
    local_states = jnp.einsum(
        "hce,ehpn->chpn", link_weight, block_states, precision=lax.Precision.HIGHEST
    )
    summary = local_states[blocks]
    device_rate = prefix_rate[blocks]

    def combine(earlier_part, later_part):
        return (
            earlier_part[0] + later_part[0],
            jnp.exp(later_part[0])[:, None, None] * earlier_part[1] + later_part[1],
        )

    identity = (
        jnp.zeros((head_count,), jnp.float32),
        jnp.zeros((head_count, head_size, state_size), jnp.float32),
    )
    carried = entering((device_rate, summary), SEQ, combine, identity)[1]
    block_inputs = (
        local_states[:blocks] + jnp.exp(prefix_rate[:blocks])[:, :, None, None] * carried[None]
    )
    cross_out = jnp.exp(running)[..., None] * jnp.einsum(
        "ctn,chpn->cthp",
        values_c.astype(jnp.float32),
        block_inputs,
        precision=lax.Precision.HIGHEST,
    )
    mixer_out = (intra_out + cross_out + skip_gain[:, None] * values_x.astype(jnp.float32)).reshape(
        seq_rows, local_width
    )
    gated = mixer_out * jax.nn.silu(gate_in.astype(jnp.float32))
    squares = taken_together(jnp.sum(gated * gated, axis=1), "head")
    inverse_rms = lax.rsqrt(squares / (local_width * lax.axis_size("head")) + norm_floor)
    normed_out = (gated * inverse_rms[:, None] * norm_gain).astype(jnp.bfloat16)
    mixed = summed_on_arrival(
        jnp.dot(normed_out, out_proj, preferred_element_type=jnp.float32).astype(jnp.bfloat16),
        "head",
        0,
    )
    return mixed.astype(jnp.bfloat16)


def solution(mesh):
    finer = Mesh(mesh.devices.reshape(4, 8, mesh.shape["head"]), ("seq_0", "seq_1", "head"))
    in_specs = (
        P(SEQ_HEAD, None),
        P(),
        P(None, None, "head"),
        P(),
        P(None, "head"),
        P(),
        P("head"),
        P(),
        P("head"),
        P("head"),
        P("head"),
        P("head"),
        P("head", None),
    )
    out_specs = P(SEQ_HEAD, None)
    return jax.shard_map(
        on_device, mesh=finer, in_specs=in_specs, out_specs=out_specs, check_vma=False
    )
```

profile of v0, /device:TPU:16, one launch (start us, length us, event | category | flops | bytes accessed | tf_op | source)
XLA Modules:
  0.0 238.6 jit_solution(7252940572213324971)
XLA Ops:
  7.9 2.0 fusion.18
  10.1 6.7 %copy.137 = bf16[320,8,2,640]{3,1,2,0:T(8,128)(2,1)} copy(bf16[320,8,2,640]{3,2,1,0:T(2,128)(2,1)} %bitcast.167) | data formatting | bytes 13107200
  18.1 28.3 %all-gather.5.cloned.1.call-done = bf16[768,2560]{1,0:T(8,128)(2,1)} async-done(((bf16[96,2560]{1,0:T(8,128)(2,1)}), bf16[768,2560]{1,0:T(8,128)(2,1)}) %all-gather.5.cloned.1.call-update) | async-done | bytes 3932176 | tf_op jit(solution)/shard_map/all_gather | solution.py:104
  46.4 5.3 %fusion.66 = (bf16[768,336]{0,1:T(8,128)(2,1)}, f32[768,336]{0,1:T(8,128)}) fusion(bf16[768,2560]{1,0:T(8,128)(2,1)} %all-gather.5.cloned.1.call-done, bf16[2560,336]{0,1:T(8,128)(2,1)} %param.16), kind=kOutput, calls=%fused_computation.144 | convolution fusion | flops 1321463808 | bytes 7200768 | tf_op jit(solution)/shard_map/dot_general | solution.py:106
  51.7 2.1 copy.111
  53.8 8.9 %convolution_convert_fusion.1 = bf16[768,1280]{1,0:T(8,128)(2,1)S(1)} fusion(bf16[768,2560]{1,0:T(8,128)(2,1)} %all-gather.5.cloned.1.call-done, bf16[2560,1280]{1,0:T(8,128)(2,1)} %bitcast.168), kind=kOutput, calls=%fused_computation.9 | convolution fusion | flops 5034147840 | bytes 12451840 | tf_op jit(solution)/shard_map/dot_general | solution.py:105
  68.7 3.5 %collective-permute-start = (bf16[3,896]{1,0:T(4,128)(2,1)}, bf16[3,896]{1,0:T(4,128)(2,1)S(1)}, u32[]{:S(2)}, u32[]{:S(2)}) collective-permute-start(bf16[3,896]{1,0:T(4,128)(2,1)} %pad_maximum_fusion.2), channel_id=1, source_target_pairs={{0,8},{8,16},{16,24},{24,32},{32,40},{40,48},{48,56},{56,64},{64,7... | collective-permute-start | bytes 16136 | tf_op jit(solution)/shard_map/ppermute | solution.py:18
  76.5 5.0 %multiply_convert_fusion.2 = bf16[768,896]{1,0:T(8,128)(2,1)S(1)} fusion(bf16[768,896]{1,0:T(8,128)(2,1)} %pad_maximum_fusion.1, bf16[3,896]{1,0:T(4,128)(2,1)S(1)} %collective-permute-done, f32[896]{0:T(1024)S(1)} %get-tuple-element.6, f32[896]{0:T(1024)S(1)} %get-tuple-element.7, f32[896]{0:T(1024)S(1)} %get-tuple-element.8, f32[896]{0:T(1024)S(1)} %get-tuple-element.5, ...), kind=kLoop, calls=%fused_computation.10 | loop fusion | flops 17891328 | bytes 2775808 | tf_op jit(solution)/shard_map/convert_element_type | solution.py:124
  83.3 2.3 copy.112
  85.6 3.8 %reshape.237 = bf16[3,256,10,64]{1,0,3,2:T(4,128)(2,1)} reshape(bf16[768,640]{0,1:T(8,128)(2,1)} %copy.112) | data formatting | bytes 1966080 | tf_op jit(solution)/shard_map/reshape | solution.py:126
  91.1 2.8 %convolution_bitcast_fusion = f32[4,10,64,128]{3,0,2,1:T(4,128)S(1)} fusion(f32[3,10,64,128]{3,2,1,0:T(8,128)S(1)} %fusion.19, f32[10,3]{1,0:T(8,128)S(1)} %copy-done.14, f32[10,4]{1,0:T(8,128)S(1)} %copy-done.13, pred[4,3]{1,0:T(4,128)(4,1)S(1)} %copy-done.27), kind=kOutput, calls=%fused_computation.26 | convolution fusion | flops 11796840 | bytes 2294052 | tf_op jit(solution)/shard_map/hce,ehpn->chpn/dot_general | solution.py:162
  98.2 14.5 %all-gather = bf16[8,1,10]{2,1,0:T(2,128)(2,1)S(1)} all-gather(bf16[1,1,10]{2,1,0:T(2,128)(2,1)S(1)} %slice_bitcast_fusion.5), channel_id=1, replica_groups=mesh['seq_0'=4,'seq_1'=8,'head'=8] {'seq_1'}, dimensions={0}, use_global_device_ids=true | all-gather | bytes 180 | tf_op jit(solution)/shard_map/all_gather | solution.py:33
  113.8 8.1 %all-gather.1 = bf16[4,1,10]{2,1,0:T(2,128)(2,1)} all-gather(bf16[1,1,10]{2,1,0:T(2,128)(2,1)S(1)} %get-tuple-element.17), channel_id=1, replica_groups=mesh['seq_0'=4,'seq_1'=8,'head'=8] {'seq_0'}, dimensions={0}, use_global_device_ids=true | all-gather | bytes 100 | tf_op jit(solution)/shard_map/all_gather | solution.py:33
  126.7 2.1 fusion.67
  128.8 5.6 %all-gather.7.cloned.1.call-done = bf16[8,10,64,128]{3,2,1,0:T(8,128)(2,1)} async-done(((bf16[1,10,64,128]{3,2,1,0:T(8,128)(2,1)}), bf16[8,10,64,128]{3,2,1,0:T(8,128)(2,1)}) %all-gather.7.cloned.1.call-update) | async-done | bytes 1310736 | tf_op jit(solution)/shard_map/all_gather | solution.py:33
  134.4 1.9 fusion.28
  136.3 11.8 %all_gather.23 = bf16[4,10,64,128]{3,2,1,0:T(8,128)(2,1)S(1)} all-gather(bf16[1,10,64,128]{3,2,1,0:T(8,128)(2,1)S(1)} %fusion.28), channel_id=1, replica_groups=mesh['seq_0'=4,'seq_1'=8,'head'=8] {'seq_0'}, dimensions={0}, use_global_device_ids=true | all-gather | bytes 819200 | tf_op jit(solution)/shard_map/all_gather | solution.py:33
  151.2 2.7 %fusion.8 = f32[3,256,10,64]{1,3,2,0:T(8,128)S(1)} fusion(f32[3,256,10,64]{1,3,2,0:T(8,128)S(1)} %fusion.21, f32[3,10,256]{2,1,0:T(8,128)S(1)} %copy-done.11, f32[3,10,256]{2,1,0:T(8,128)S(1)} %copy-done.9, f32[3,256,256]{2,1,0:T(8,128)S(1)} %copy-done.7, pred[256,256]{1,0:T(8,128)(4,1)S(1)} %copy-done.8, f32[10]{0:T(128)S(1)} %copy-done.30, ...), kind=kOutput, calls=%fused_computation.16 | convolution fusion | flops 265912320 | bytes 5859368 | tf_op jit(solution)/shard_map/chts,cshp->cthp/dot_general | solution.py:144
  157.0 2.8 %copy.131 = f32[768,640]{1,0:T(8,128)} copy(f32[768,640]{0,1:T(8,128)} %bitcast.166) | data formatting | bytes 3932160 | tf_op jit(solution)/shard_map/reshape | solution.py:188
  159.9 2.5 %multiply_reduce_fusion = f32[768]{0:T(1024)S(1)} fusion(f32[768,640]{1,0:T(8,128)} %copy.131, bf16[768,1280]{1,0:T(8,128)(2,1)} %copy-done.1), kind=kLoop, calls=%fused_computation.23 | loop fusion | flops 3931392 | bytes 2952192 | tf_op jit(solution)/shard_map/reduce_sum | solution.py:192
  162.4 9.5 %all_to_all.11 = f32[8,1,768]{2,1,0:T(1,128)S(1)} all-to-all(f32[8,1,768]{2,1,0:T(1,128)S(1)} %broadcast_in_dim.36), channel_id=1, replica_groups=mesh['seq_0'=4,'seq_1'=8,'head'=8] {'head'}, dimensions={0} | all-to-all | bytes 49152 | tf_op jit(solution)/shard_map/all_to_all | solution.py:50
  171.9 6.2 %convolution_convert_fusion = bf16[768,2560]{1,0:T(8,128)(2,1)S(1)} fusion(bf16[640,2560]{1,0:T(8,128)(2,1)S(1)} %copy-done, f32[640]{0:T(1024)S(1)} %copy-done.28, f32[768]{0:T(1024)S(1)} %add_rsqrt_fusion, f32[768,640]{1,0:T(8,128)} %copy.131, bf16[768,1280]{1,0:T(8,128)(2,1)} %copy-done.1), kind=kOutput, calls=%fused_computation.1 | convolution fusion | flops 2522972160 | bytes 10163712 | tf_op jit(solution)/shard_map/dot_general | solution.py:196
  178.1 50.1 %all_to_all.12 = bf16[8,96,2560]{2,1,0:T(8,128)(2,1)} all-to-all(bf16[8,96,2560]{2,1,0:T(8,128)(2,1)S(1)} %bitcast.169), channel_id=1, replica_groups=mesh['seq_0'=4,'seq_1'=8,'head'=8] {'head'}, dimensions={0} | all-to-all | bytes 7864320 | tf_op jit(solution)/shard_map/all_to_all | solution.py:67
  228.2 3.6 %reduce_sum.42 = bf16[96,2560]{1,0:T(8,128)(2,1)} reduce(bf16[8,96,2560]{2,1,0:T(8,128)(2,1)} %all_to_all.12, bf16[]{:T(256)} %constant.60.clone.1), dimensions={0}, to_apply=%region_6.7 | reduce | flops 1720320 | bytes 4423682 | tf_op jit(solution)/shard_map/reduce_sum | solution.py:68
  (124 shorter events, 32.6 us)
Async XLA Ops:
  6.5 165.3 %copy-start = (bf16[640,2560]{1,0:T(8,128)(2,1)S(1)}, bf16[640,2560]{1,0:T(8,128)(2,1)}, u32[]{:S(2)}) copy-start(bf16[640,2560]{1,0:T(8,128)(2,1)} %param.25) | copy-start | bytes 9830404
  6.5 39.8 %all-gather.5.cloned.1.call-start = ((), (), s32[]{:S(2)}) async-start(), calls=%async_computation.2 | async-start | bytes 4423680 | tf_op jit(solution)/shard_map/all_gather | solution.py:104
  10.0 124.5 %all-gather.7.cloned.1.call-start = ((), (), s32[]{:S(2)}) async-start(), calls=%async_computation.3 | async-start | bytes 1474560 | tf_op jit(solution)/shard_map/all_gather | solution.py:33
  10.0 7.4 %copy-start.16 = (f32[4,640]{1,0:T(4,128)S(1)}, f32[4,640]{1,0:T(4,128)}, u32[]{:S(2)}) copy-start(f32[4,640]{1,0:T(4,128)} %param.17) | copy-start | bytes 30724
  10.0 7.4 %copy-start.22 = (f32[4,256]{1,0:T(4,128)S(1)}, f32[4,256]{1,0:T(4,128)}, u32[]{:S(2)}) copy-start(f32[4,256]{1,0:T(4,128)} %param.18) | copy-start | bytes 12292
  10.0 7.4 %copy-start.23 = (f32[640]{0:T(1024)S(1)}, f32[640]{0:T(1024)}, u32[]{:S(2)}) copy-start(f32[640]{0:T(1024)} %param.19) | copy-start | bytes 7684
  10.1 7.4 %copy-start.25 = (f32[256]{0:T(256)S(1)}, f32[256]{0:T(256)}, u32[]{:S(2)}) copy-start(f32[256]{0:T(256)} %param.20) | copy-start | bytes 3076
  10.1 8.0 %copy-start.29 = (f32[10]{0:T(128)S(1)}, f32[10]{0:T(128)}, u32[]{:S(2)}) copy-start(f32[10]{0:T(128)} %param.22) | copy-start | bytes 124
  53.8 8.9 %copy-start.4 = (bf16[768,336]{1,0:T(8,128)(2,1)S(1)}, bf16[768,336]{1,0:T(8,128)(2,1)}, u32[]{:S(2)}) copy-start(bf16[768,336]{1,0:T(8,128)(2,1)} %copy.111) | copy-start | bytes 1548292
  68.7 7.9 %copy-start.15 = (f32[3,10]{1,0:T(4,128)}, f32[3,10]{1,0:T(4,128)S(1)}, u32[]{:S(2)}) copy-start(f32[3,10]{1,0:T(4,128)S(1)} %reduce_window_sum.36) | copy-start | bytes 364
  68.7 7.9 %collective-permute-start = (bf16[3,896]{1,0:T(4,128)(2,1)}, bf16[3,896]{1,0:T(4,128)(2,1)S(1)}, u32[]{:S(2)}, u32[]{:S(2)}) collective-permute-start(bf16[3,896]{1,0:T(4,128)(2,1)} %pad_maximum_fusion.2), channel_id=1, source_target_pairs={{0,8},{8,16},{16,24},{24,32},{32,40},{40,48},{48,56},{56,64},{64,7... | collective-permute-start | bytes 16136 | tf_op jit(solution)/shard_map/ppermute | solution.py:18
  89.3 1.8 copy-start.13
  89.3 1.8 copy-start.14
  89.3 1.8 copy-start.27
  112.6 10.0 %copy-start.12 = (bf16[8,1,10]{2,1,0:T(2,128)(2,1)}, bf16[8,1,10]{2,1,0:T(2,128)(2,1)S(1)}, u32[]{:S(2)}) copy-start(bf16[8,1,10]{2,1,0:T(2,128)(2,1)S(1)} %all-gather) | copy-start | bytes 484
  122.6 25.6 %copy-start.17 = (f32[10]{0:T(128)S(1)}, f32[10]{0:T(128)}, u32[]{:S(2)}) copy-start(f32[10]{0:T(128)} %get-tuple-element.18) | copy-start | bytes 124
  122.6 25.6 %copy-start.18 = (f32[10]{0:T(128)S(1)}, f32[10]{0:T(128)}, u32[]{:S(2)}) copy-start(f32[10]{0:T(128)} %get-tuple-element.19) | copy-start | bytes 124
  122.6 25.6 %copy-start.19 = (f32[10]{0:T(128)S(1)}, f32[10]{0:T(128)}, u32[]{:S(2)}) copy-start(f32[10]{0:T(128)} %get-tuple-element.20) | copy-start | bytes 124
  122.6 25.6 %copy-start.20 = (f32[10]{0:T(128)S(1)}, f32[10]{0:T(128)}, u32[]{:S(2)}) copy-start(f32[10]{0:T(128)} %get-tuple-element.21) | copy-start | bytes 124
  122.6 25.6 %copy-start.21 = (f32[10]{0:T(128)S(1)}, f32[10]{0:T(128)}, u32[]{:S(2)}) copy-start(f32[10]{0:T(128)} %get-tuple-element.22) | copy-start | bytes 124
  125.4 22.8 %copy-start.24 = (f32[10]{0:T(128)S(1)}, f32[10]{0:T(128)}, u32[]{:S(2)}) copy-start(f32[10]{0:T(128)} %get-tuple-element.9) | copy-start | bytes 124
  134.4 13.8 %copy-start.5 = (bf16[8,10,64,128]{3,2,1,0:T(8,128)(2,1)S(1)}, bf16[8,10,64,128]{3,2,1,0:T(8,128)(2,1)}, u32[]{:S(2)}) copy-start(bf16[8,10,64,128]{3,2,1,0:T(8,128)(2,1)} %all-gather.7.cloned.1.call-done) | copy-start | bytes 3932164
  134.4 14.8 %copy-start.3 = (f32[4,10,64,128]{3,0,2,1:T(4,128)S(1)}, f32[4,10,64,128]{3,0,2,1:T(4,128)}, u32[]{:S(2)}) copy-start(f32[4,10,64,128]{3,0,2,1:T(4,128)} %copy-done.2) | copy-start | bytes 3932164
  159.9 12.0 %copy-start.28 = (f32[640]{0:T(1024)S(1)}, f32[640]{0:T(1024)}, u32[]{:S(2)}) copy-start(f32[640]{0:T(1024)} %param.24) | copy-start | bytes 7684
  (10 other events, 14.7 us)
Sparse Core Ops, SparseCore 0:
  10.1 36.2 all-gather.4
  96.2 38.1 all-gather.6
where the time goes:
time: 242 us; the launch traced here: 239 us
  blocking collectives  94 us (39%)
  waiting for transfers between devices  35.7 us (15%)
  local copies, waits for them, and re-layouts  32.7 us (14%)
  matrix products  30.8 us (13%)
  other arithmetic  27.9 us (12%)
  between operations  13.9 us (6%)
  starting transfers between devices  3.5 us (1%)
    all_to_all x1, blocking collectives, summed_on_arrival(): lax.all_to_all(pieces, axis, split_axis=0, concat_axis=0, tiled=True)  50.1 us
    all_gather x3, blocking collectives, entering(): lax.all_gather(part.astype(kind), axis)  34.4 us
    all_gather x1, waiting for transfers between devices, on_device(): normed = lax.all_gather(own_normed, 'head', axis=0, tiled=True)  28.3 us
    unnamed x66, local copies, waits for them, and re-layouts  10.6 us
    all_to_all x1, blocking collectives, from_everyone(): lax.all_to_all(jnp.broadcast_to(array[None], (length, *array.shape)), axi...  9.46 us
    dot_general x1, matrix products, on_device(): jnp.dot(normed, joined_proj, preferred_element_type=jnp.float32)  8.93 us
    dot_general x1, matrix products, on_device(): jnp.dot(normed_out, out_proj, preferred_element_type=jnp.float32)  6.16 us
    all_gather x1, waiting for transfers between devices, entering(): lax.all_gather(part.astype(kind), axis)  5.58 us
  transfers between devices with their start and end apart: 3, of which 3 were waited for; matrix products, arithmetic and copies ran while one was open for 9% of the time, Pallas kernels for 0%

commit v1 on v0

v1 whole, which is shorter than its diff:
```python
import functools

import jax
import jax.numpy as jnp
from jax import lax
from jax.experimental import pallas as pl
from jax.experimental.pallas import tpu as pltpu
from jax.sharding import PartitionSpec as P

MESH = pl.DeviceIdType.MESH
BF16 = jnp.bfloat16
F32 = jnp.float32

NORM_FLOOR = 0.1
D = 2560
DL = 640
NS = 128
R = 96
HALF = 48
T = 768
Q = 128
NQ = 6
CH = 192
HEADS = 10
NY, NZ, NX = 4, 8, 4


def dot(a, b):
    return jnp.dot(a, b, preferred_element_type=F32)


def dot_t(a, b):
    return lax.dot_general(a, b, (((1,), (1,)), ((), ())), preferred_element_type=F32)


def t_dot(a, b):
    return lax.dot_general(a, b, (((0,), (0,)), ((), ())), preferred_element_type=F32)


def split2(v):
    hi = v.astype(BF16)
    lo = (v - hi.astype(F32)).astype(BF16)
    return hi, lo


def split3(v):
    hi, mid = split2(v)
    lo = (v - hi.astype(F32) - mid.astype(F32)).astype(BF16)
    return hi, mid, lo


def silu(v):
    return v / (1.0 + jnp.exp(-v))


def remote(src, dst, send, recv, device):
    return pltpu.make_async_remote_copy(
        src_ref=src, dst_ref=dst, send_sem=send, recv_sem=recv, device_id=device, device_id_type=MESH
    )


def kernel(
    tokens, pre_gain, w_hbm, wo_hbm, kernel_x, kernel_bc, offset_x, offset_bc, dt_bias, a_log,
    skip_gain, norm_gain, wout_hbm,
    out,
    w, wo, wout, rows, xin, dtr, zs, xb, bmat, cmat, dts, cum, expand, ef, sl, sacc, pdr, pdacc,
    yv, sb, drow, rz, rd, pz, pdz, tb, tdb, ty, tdy, cacc, pb, cr, gb, sqc, part, pr, ps, rl, rf,
    sqs, sqr, small,
    ag_s, ag_r, halo_s, halo_r, zs_s, zs_r, zd_s, zd_r, y_s, y_r, yd_s, yd_r, bk_s, bk_r,
    pp_s, pp_r, rl_s, rl_r, rf_s, rf_r, sq_s, sq_r, w_s,
):
    s = lax.axis_index("seq")
    h = lax.axis_index("head")
    y = s // NZ
    z = s % NZ
    x = h // 2
    c = h % 2
    partner = x * 2 + (1 - c)
    xr = (x + 1) % NX
    xl = (x + NX - 1) % NX
    xo = (x + 2) % NX
    hr, hl, ho = xr * 2 + c, xl * 2 + c, xo * 2 + c

    w_copies = [
        pltpu.make_async_copy(w_hbm, w, w_s.at[0]),
        pltpu.make_async_copy(wo_hbm, wo, w_s.at[1]),
        pltpu.make_async_copy(wout_hbm, wout, w_s.at[2]),
    ]
    for cp in w_copies:
        cp.start()

    barrier = pltpu.get_barrier_semaphore()
    for k in range(1, 8):
        pl.semaphore_signal(barrier, inc=1, device_id=(s, (h + k) % 8), device_id_type=MESH)
    for k in range(1, NZ):
        pl.semaphore_signal(barrier, inc=1, device_id=(y * NZ + (z + k) % NZ, h), device_id_type=MESH)
    for k in range(1, NY):
        pl.semaphore_signal(barrier, inc=1, device_id=(((y + k) % NY) * NZ + z, h), device_id_type=MESH)
    for k in (1, 31):
        pl.semaphore_signal(barrier, inc=1, device_id=((s + k) % 32, h), device_id_type=MESH)

    for half in range(2):
        tk = tokens[half * HALF : (half + 1) * HALF, :].astype(F32)
        inv = lax.rsqrt(jnp.mean(tk * tk, axis=1, keepdims=True) + NORM_FLOOR)
        rows[h, half] = (tk * inv * pre_gain[...]).astype(BF16)

    pl.semaphore_wait(barrier, 19)

    def ag(origin, half, role, device):
        return remote(
            rows.at[origin, half], rows.at[origin, half], ag_s.at[role], ag_r.at[role], (s, device)
        )

    own_pair = remote(rows.at[h], rows.at[h], ag_s.at[6], ag_r.at[6], (s, partner))
    sends = [ag(h, 0, 0, hr), ag(h, 1, 3, hl), ag(h, 1, 1, hr), ag(h, 0, 2, hl)]
    own_pair.start()
    for cp in sends:
        cp.start()

    li = lax.broadcasted_iota(jnp.int32, (2 * Q, DL), 0)
    lc = lax.broadcasted_iota(jnp.int32, (2 * Q, DL), 1)
    head_of = lax.shift_right_logical(lc, 6)
    expand[...] = jnp.where(jnp.bitwise_and(li, Q - 1) == head_of, 1.0, 0.0).astype(BF16)
    small[...] = jnp.zeros_like(small)
    small[0:1, 0:HEADS] = dt_bias[...]
    small[1:2, 0:HEADS] = a_log[...]
    small[2:3, 0:HEADS] = skip_gain[...]
    dtr[...] = jnp.zeros_like(dtr)
    for cp in w_copies:
        cp.wait()

    def project(chip, with_x, with_z):
        n = rows[pl.ds(2 * chip, 2)].reshape(CH, D)
        at = pl.multiple_of(chip * CH, CH)
        if with_x:
            xin[pl.ds(pl.multiple_of(at + 8, 8), CH), 0:DL] = dot(n, w[1]).astype(BF16).astype(F32)
            xin[pl.ds(pl.multiple_of(at + 8, 8), CH), DL : DL + 2 * NS] = (
                dot_t(n, wo[0 : 2 * NS, :]).astype(BF16).astype(F32)
            )
            dtr[pl.ds(at, CH), 0:80] = dot_t(n, wo[2 * NS : 2 * NS + 80, :])
        if with_z:
            zz = dot(n, w[0]).astype(BF16).astype(F32)
            zs[pl.ds(at, CH), :] = silu(zz)

    remote(rows.at[partner], rows.at[partner], ag_s.at[6], ag_r.at[6], (s, partner)).wait_recv()
    project(x, True, True)

    def to_partner(origin, half, role):
        cp = ag(origin, half, 7 + role, partner)
        cp.start()
        sends.append(cp)

    def partner_done(chip, half, role):
        ag(chip * 2 + 1 - c, half, 7 + role, partner).wait_recv()

    ag(hl, 0, 0, hr).wait_recv()
    cp = ag(hl, 0, 4, hr)
    cp.start()
    sends.append(cp)
    ag(hr, 1, 3, hl).wait_recv()
    cp = ag(hr, 1, 5, hl)
    cp.start()
    sends.append(cp)
    to_partner(hl, 0, 0)
    to_partner(hr, 1, 3)
    ag(hl, 1, 1, hr).wait_recv()
    to_partner(hl, 1, 1)
    ag(hr, 0, 2, hl).wait_recv()
    to_partner(hr, 0, 2)
    partner_done(xl, 0, 0)
    partner_done(xl, 1, 1)
    project(xl, True, True)
    partner_done(xr, 1, 3)
    partner_done(xr, 0, 2)
    project(xr, True, True)
    ag(ho, 0, 4, hr).wait_recv()
    to_partner(ho, 0, 4)
    ag(ho, 1, 5, hl).wait_recv()
    to_partner(ho, 1, 5)
    partner_done(xo, 0, 4)
    partner_done(xo, 1, 5)
    project(xo, True, False)

    halo = remote(xin.at[pl.ds(T, 8)], xin.at[pl.ds(0, 8)], halo_s, halo_r, ((s + 1) % 32, h))

    @pl.when(s < 31)
    def _():
        halo.start()

    lane = lax.broadcasted_iota(jnp.int32, (1, Q), 1)
    ri = lax.broadcasted_iota(jnp.int32, (Q, Q), 0)
    ci = lax.broadcasted_iota(jnp.int32, (Q, Q), 1)
    tri = jnp.where(ri >= ci, 1.0, 0.0).astype(BF16)
    bias_row = small[0:1, :]
    rate_row = -jnp.exp(small[1:2, :])
    shift = (Q - h * HEADS) % Q
    total = jnp.zeros((1, Q), F32)
    for q in range(NQ):
        raw = pltpu.roll(dtr[q * Q : (q + 1) * Q, :], shift, 1) + bias_row
        step = jnp.maximum(raw, 0.0) + jnp.log1p(jnp.exp(-jnp.abs(raw)))
        step = jnp.where(lane < HEADS, step, 0.0)
        la = step * rate_row
        dts[q] = step
        p3 = dot(tri, jnp.concatenate(split3(la), axis=1))
        cq = p3[:, 0:Q] + p3[:, Q : 2 * Q] + p3[:, 2 * Q : 3 * Q]
        cum[q] = cq
        total = total + cq[Q - 1 : Q, :]
    drow[...] = jnp.broadcast_to(jnp.exp(total), (8, Q))
    rd[z] = drow[...]

    def z_peer(k):
        return (z + k) % NZ

    for k in range(1, NZ):
        zp = z_peer(k)
        remote(drow, rd.at[z], zd_s.at[k], zd_r.at[z], (y * NZ + zp, h)).start()

    def conv_block(i):
        at = pl.multiple_of(i * 64, 64)
        for lo, hi, kern, off in ((0, DL, kernel_x, offset_x), (DL, DL + 2 * NS, kernel_bc, offset_bc)):
            u = jnp.broadcast_to(off[...], (64, hi - lo))
            v = xin[pl.ds(at, 72), lo:hi]
            for k in range(4):
                u = u + kern[k : k + 1, :] * v[5 + k : 69 + k, :]
            v = silu(u).astype(BF16)
            if lo == 0:
                xb[pl.ds(at, 64), :] = v
            else:
                bmat[pl.ds(at, 64), :] = v[:, 0:NS]
                cmat[pl.ds(at, 64), :] = v[:, NS : 2 * NS]

    def conv_step(i, carry):
        conv_block(i)
        return carry

    lax.fori_loop(1, T // 64, conv_step, 0)

    @pl.when(s == 0)
    def _():
        xin[0:8, :] = jnp.zeros((8, DL + 2 * NS), F32)

    @pl.when(s > 0)
    def _():
        halo.wait_recv()

    conv_block(0)

    sacc[...] = jnp.zeros_like(sacc)
    pdacc[...] = jnp.ones_like(pdacc)

    def state_step(q, carry):
        at = pl.multiple_of(q * Q, Q)
        cq = cum[q]
        fac = jnp.exp(cq[Q - 1 : Q, :] - cq) * dts[q]
        fx = dot(jnp.concatenate(split2(fac), axis=1), expand[...])
        ex = dot(jnp.concatenate(split2(jnp.exp(cq)), axis=1), expand[...])
        ef[q] = ex
        xw = (xb[pl.ds(at, Q), :].astype(F32) * fx).astype(BF16)
        st = t_dot(bmat[pl.ds(at, Q), :], xw)
        dec = ex[Q - 1 : Q, :]
        prev = sacc[...]
        sl[q] = prev
        sacc[...] = prev * dec + st
        pdr[q] = pdacc[...]
        pdacc[...] = pdacc[...] * dec
        return carry

    lax.fori_loop(0, NQ, state_step, 0)
    sb[...] = sacc[...].astype(BF16)
    rz[z] = sb[pl.ds(pl.multiple_of(z * 16, 16), 16), :]

    for k in range(1, NZ):
        zp = z_peer(k)
        remote(
            sb.at[pl.ds(pl.multiple_of(zp * 16, 16), 16)], rz.at[z], zs_s.at[k], zs_r.at[z],
            (y * NZ + zp, h),
        ).start()

    project(xo, False, True)
    s3 = jnp.concatenate(split2(jnp.broadcast_to(small[2:3, :], (8, Q))), axis=1)
    skip_row = dot(s3, expand[...])[0:1, :]
    low = lax.broadcasted_iota(jnp.int32, (Q, Q), 1) < 64

    def intra_step(q, carry):
        at = pl.multiple_of(q * Q, Q)
        cq = cum[q]
        cqt = jnp.transpose(cq)
        dtt = jnp.transpose(dts[q])
        cb = dot_t(cmat[pl.ds(at, Q), :], bmat[pl.ds(at, Q), :])
        cbm = jnp.where(ri >= ci, cb, 0.0)
        for j in range(HEADS // 2):
            mixes = []
            for hh in (2 * j, 2 * j + 1):
                gap = jnp.minimum(cq[:, hh : hh + 1] - cqt[hh : hh + 1, :], 0.0)
                mixes.append((cbm * jnp.exp(gap) * dtt[hh : hh + 1, :]).astype(BF16))
            xp = xb[pl.ds(at, Q), j * Q : (j + 1) * Q].astype(F32)
            xd = jnp.concatenate(
                [jnp.where(low, xp, 0.0).astype(BF16), jnp.where(low, 0.0, xp).astype(BF16)], axis=0
            )
            yq = dot(jnp.concatenate(mixes, axis=1), xd)
            yv[pl.ds(at, Q), j * Q : (j + 1) * Q] = yq + skip_row[:, j * Q : (j + 1) * Q] * xp
        return carry

    lax.fori_loop(0, NQ, intra_step, 0)

    for k in range(1, NZ):
        zp = z_peer(k)
        remote(drow, rd.at[zp], zd_s.at[k], zd_r.at[zp], (y * NZ + zp, h)).wait_recv()
        remote(sb.at[pl.ds(0, 16)], rz.at[zp], zs_s.at[k], zs_r.at[zp], (y * NZ + zp, h)).wait_recv()
    dz = jnp.concatenate([rd[k][0:1, :] for k in range(NZ)], axis=0)
    dx = dot(jnp.concatenate(split2(dz), axis=1), expand[...])
    acc = jnp.zeros((16, DL), F32)
    pd = jnp.ones((1, DL), F32)
    for k in range(NZ):
        pz[k] = acc
        pdz[k] = jnp.broadcast_to(pd, (8, DL))
        acc = acc * dx[k : k + 1, :] + rz[k].astype(F32)
        pd = pd * dx[k : k + 1, :]
    tb[...] = acc.astype(BF16)
    tdb[...] = jnp.broadcast_to(pd, (8, DL))

    for k in range(1, NY):
        @pl.when(y + k < NY)
        def _(k=k):
            dev = ((y + k) % NY * NZ + z, h)
            remote(tb, ty.at[y], y_s.at[k], y_r.at[y], dev).start()
            remote(tdb, tdy.at[y], yd_s.at[k], yd_r.at[y], dev).start()

    cacc[...] = jnp.zeros_like(cacc)
    for k in range(NY - 1):
        @pl.when(k < y)
        def _(k=k):
            dev = (k * NZ + z, h)
            remote(tb, ty.at[k], y_s.at[1], y_r.at[k], dev).wait_recv()
            remote(tdb, tdy.at[k], yd_s.at[1], yd_r.at[k], dev).wait_recv()
            cacc[...] = cacc[...] * tdy[k][0:1, :] + ty[k].astype(F32)

    for k in range(NZ):
        pb[k] = (pz[k] + pdz[k][0:1, :] * cacc[...]).astype(BF16)
    cr[z] = pb[z]
    for k in range(1, NZ):
        zp = z_peer(k)
        remote(pb.at[zp], cr.at[z], bk_s.at[k], bk_r.at[z], (y * NZ + zp, h)).start()
    for k in range(1, NZ):
        zp = z_peer(k)
        remote(pb.at[zp], cr.at[zp], bk_s.at[k], bk_r.at[zp], (y * NZ + zp, h)).wait_recv()

    def out_step(q, carry):
        at = pl.multiple_of(q * Q, Q)
        state = (sl[q] + pdr[q][0:1, :] * cr[...].reshape(NS, DL).astype(F32)).astype(BF16)
        cross = dot(cmat[pl.ds(at, Q), :], state)
        g = (yv[pl.ds(at, Q), :] + ef[q] * cross) * zs[pl.ds(at, Q), :]
        sqc[pl.ds(at, Q), :] = jnp.broadcast_to(jnp.sum(g * g, axis=1, keepdims=True), (Q, Q))
        gb[pl.ds(at, Q), :] = (g * norm_gain[...]).astype(BF16)
        return carry

    pair_sends = []

    def out_chip(d):
        n = gb[pl.ds(pl.multiple_of(d * CH, CH), CH), :]
        for lo in range(0, D, 512):
            part[pl.ds(2 * d, 2), :, :, lo : lo + 512] = (
                dot(n, wout[:, lo : lo + 512]).astype(BF16).reshape(2, 2, HALF, 512)
            )
        cp = remote(part.at[2 * d + 1 - c], pr.at[d], pp_s.at[d], pp_r.at[d], (s, partner))
        cp.start()
        pair_sends.append(cp)

    def pair_sum(d, half):
        return part[2 * d + c, half].astype(F32) + pr[d, half].astype(F32)

    def pair_wait(d):
        remote(part.at[0], pr.at[d], pp_s.at[d], pp_r.at[d], (s, partner)).wait_recv()

    first = xo // 2
    d1 = xo + 1 - 2 * (xo % 2)
    d2 = x + 1 - 2 * (x % 2)
    lax.fori_loop(first * 3, first * 3 + 3, out_step, 0)
    out_chip(xo)
    out_chip(d1)
    pair_wait(xo)
    for half in range(2):
        ps[0, half] = pair_sum(xo, half).astype(BF16)
    relays = [
        remote(ps.at[0, 0], rl.at[0], rl_s.at[0], rl_r.at[0], (s, hr)),
        remote(ps.at[0, 1], rl.at[1], rl_s.at[1], rl_r.at[1], (s, hl)),
    ]
    for cp in relays:
        cp.start()

    def side_of(d):
        return jnp.where(d == xr, 0, 1)

    finals = []

    def final_send(slot, d, half):
        side = side_of(d)
        cp = remote(
            ps.at[slot, half], rf.at[side, half], rf_s.at[side, half], rf_r.at[side, half], (s, 2 * d + c)
        )
        cp.start()
        finals.append(cp)

    def send_direct(slot, d):
        half = 1 - side_of(d)
        pair_wait(d)
        ps[slot, half] = pair_sum(d, half).astype(BF16)
        final_send(slot, d, half)

    def send_relayed(slot, d):
        half = side_of(d)
        remote(ps.at[0, 0], rl.at[half], rl_s.at[half], rl_r.at[half], (s, hr)).wait_recv()
        ps[slot, half] = (pair_sum(d, half) + rl[half].astype(F32)).astype(BF16)
        final_send(slot, d, half)

    send_direct(1, d1)
    second = x // 2
    lax.fori_loop(second * 3, second * 3 + 3, out_step, 0)
    out_chip(d2)
    send_direct(2, d2)
    send_relayed(1, d1)
    send_relayed(2, d2)
    out_chip(x)

    sq_sends = []
    for k in range(8):
        col = sqc[pl.ds(pl.multiple_of(((h + k) % 8) * R, 32), Q), :]
        sqs[(h + k) % 8] = jnp.transpose(col)[0:8, :]
        if k == 0:
            sqr[h] = sqs[h]
        else:
            cp = remote(sqs.at[(h + k) % 8], sqr.at[h], sq_s.at[k], sq_r.at[h], (s, (h + k) % 8))
            cp.start()
            sq_sends.append(cp)
    pair_wait(x)
    for k in range(1, 8):
        hk = (h + k) % 8
        remote(sqs.at[0], sqr.at[hk], sq_s.at[k], sq_r.at[hk], (s, hk)).wait_recv()
    squares = jnp.sum(sqr[...], axis=0)[0:1, :]
    inv_row = lax.rsqrt(squares / (DL * 8) + NORM_FLOOR)
    inv_col = jnp.transpose(jnp.broadcast_to(inv_row, (Q, Q)))
    for half in range(2):
        for side in range(2):
            remote(
                ps.at[1, half], rf.at[side, half], rf_s.at[side, half], rf_r.at[side, half], (s, hl)
            ).wait_recv()
    for half in range(2):
        tot = pair_sum(x, half) + rf[0, half].astype(F32) + rf[1, half].astype(F32)
        out[half * HALF : (half + 1) * HALF, :] = (
            tot * inv_col[half * HALF : (half + 1) * HALF, 0:1]
        ).astype(BF16)

    own_pair.wait_send()
    for cp in sends + pair_sends + relays + finals + sq_sends:
        cp.wait_send()

    @pl.when(s < 31)
    def _():
        halo.wait_send()

    for k in range(1, NZ):
        zp = z_peer(k)
        dev = (y * NZ + zp, h)
        remote(drow, rd.at[z], zd_s.at[k], zd_r.at[z], dev).wait_send()
        remote(sb.at[pl.ds(0, 16)], rz.at[z], zs_s.at[k], zs_r.at[z], dev).wait_send()
        remote(pb.at[zp], cr.at[z], bk_s.at[k], bk_r.at[z], dev).wait_send()
    for k in range(1, NY):
        @pl.when(y + k < NY)
        def _(k=k):
            dev = ((y + k) % NY * NZ + z, h)
            remote(tb, ty.at[y], y_s.at[k], y_r.at[y], dev).wait_send()
            remote(tdb, tdy.at[y], yd_s.at[k], yd_r.at[y], dev).wait_send()


def on_device(
    tokens, pre_gain, inner_proj, outer_proj, kernel_x, kernel_bc, offset_x, offset_bc, dt_bias, a_log,
    skip_gain, norm_gain, out_proj,
):
    w = jnp.transpose(inner_proj, (1, 0, 2))
    vm = pl.BlockSpec(memory_space=pltpu.VMEM)
    hbm = pl.BlockSpec(memory_space=pl.ANY)
    dma = pltpu.SemaphoreType.DMA
    V = pltpu.VMEM
    scratch = [
        V((2, D, DL), BF16), V((336, D), BF16), V((DL, D), BF16), V((8, 2, HALF, D), BF16),
        V((T + 8, DL + 2 * NS), F32), V((T, Q), F32), V((T, DL), F32), V((T, DL), BF16),
        V((T, NS), BF16), V((T, NS), BF16), V((NQ, Q, Q), F32), V((NQ, Q, Q), F32),
        V((2 * Q, DL), BF16), V((NQ, Q, DL), F32), V((NQ, NS, DL), F32), V((NS, DL), F32),
        V((NQ, 8, DL), F32), V((8, DL), F32),
        V((T, DL), F32), V((NS, DL), BF16), V((8, Q), F32), V((NZ, 16, DL), BF16), V((NZ, 8, Q), F32),
        V((NZ, 16, DL), F32), V((NZ, 8, DL), F32), V((16, DL), BF16), V((8, DL), F32),
        V((NY, 16, DL), BF16), V((NY, 8, DL), F32), V((16, DL), F32), V((NZ, 16, DL), BF16),
        V((NZ, 16, DL), BF16), V((T, DL), BF16), V((T + 32, Q), F32), V((8, 2, HALF, D), BF16),
        V((NX, 2, HALF, D), BF16), V((3, 2, HALF, D), BF16), V((2, HALF, D), BF16), V((2, 2, HALF, D), BF16),
        V((8, 8, Q), F32), V((8, 8, Q), F32), V((8, Q), F32),
        dma((13,)), dma((13,)), dma, dma, dma((NZ,)), dma((NZ,)), dma((NZ,)), dma((NZ,)),
        dma((NY,)), dma((NY,)), dma((NY,)), dma((NY,)), dma((NZ,)), dma((NZ,)),
        dma((NX,)), dma((NX,)), dma((2,)), dma((2,)), dma((2, 2)), dma((2, 2)), dma((8,)), dma((8,)),
        dma((3,)),
    ]
    return pl.pallas_call(
        kernel,
        out_shape=jax.ShapeDtypeStruct((R, D), BF16),
        in_specs=[vm, vm, hbm, hbm, vm, vm, vm, vm, vm, vm, vm, vm, hbm],
        out_specs=vm,
        scratch_shapes=scratch,
        compiler_params=pltpu.CompilerParams(
            collective_id=0, has_side_effects=True, vmem_limit_bytes=66_000_000
        ),
    )(
        tokens, pre_gain[None], w, outer_proj.T, kernel_x, kernel_bc, offset_x[None], offset_bc[None],
        dt_bias[None], a_log[None], skip_gain[None], norm_gain[None], out_proj,
    )


def solution(mesh):
    in_specs = (
        P(("seq", "head"), None), P(), P(None, None, "head"), P(), P(None, "head"), P(), P("head"), P(),
        P("head"), P("head"), P("head"), P("head"), P("head", None),
    )
    return jax.shard_map(
        on_device, mesh=mesh, in_specs=in_specs, out_specs=P(("seq", "head"), None), check_vma=False
    )
```

time: 242 us -> 91.9 us (0.38); the launches traced: 239 us -> 91.4 us
  blocking collectives: 94 us -> 0 us
  Pallas kernels: 0 us -> 79.2 us
  waiting for transfers between devices: 35.7 us -> 0 us
  matrix products: 30.8 us -> 0 us
  other arithmetic: 27.9 us -> 0 us
  local copies, waits for them, and re-layouts: 32.7 us -> 12.1 us
  between operations: 13.9 us -> 0.01 us
  starting transfers between devices: 3.5 us -> 0 us
    pallas_call x0 -> x1, Pallas kernels: none -> 79.2 us  [on_device(): pl.pallas_call(kernel, out_shape=jax.ShapeDtypeStruct((R, D), BF16), in_s...]
    all_to_all x2 -> x0, blocking collectives: 59.6 us -> none  [the longest x1 50.1 us: summed_on_arrival(): lax.all_to_all(pieces, axis, split_axis=0, concat_axis=0, tiled=True)]
    all_gather x3 -> x0, blocking collectives: 34.4 us -> none  [entering(): lax.all_gather(part.astype(kind), axis)]
    all_gather x2 -> x0, waiting for transfers between devices: 33.9 us -> none  [the longest x1 28.3 us: on_device(): normed = lax.all_gather(own_normed, 'head', axis=0, tiled=True)]
    dot_general x8 -> x0, matrix products: 30.8 us -> none  [the longest x1 8.93 us: on_device(): jnp.dot(normed, joined_proj, preferred_element_type=jnp.float32)]
    convert_element_type x3 -> x0, other arithmetic: 8.86 us -> none  [the longest x1 4.96 us: on_device(): conv_out = jax.nn.silu(summed).astype(jnp.bfloat16)]
    reduce_sum x4 -> x0, other arithmetic: 7.47 us -> none  [the longest x1 3.57 us: summed_on_arrival(): return arrived.astype(jnp.float32).sum(axis=0)]
    slice x12 -> x0, local copies, waits for them, and re-layouts: 7.13 us -> none  [the longest x2 3.33 us: on_device(): conv_out[:, :local_width].reshape(blocks, SPAN, head_count, head_size)]
  transfers between devices with their start and end apart: 3 -> 0, of which waited for: 3 -> 0; matrix products, arithmetic and copies ran while one was open for 9% -> 0% of each run, Pallas kernels for 0% -> 0%
where the time goes in v1:
time: 91.9 us; the launch traced here: 91.4 us
  Pallas kernels  79.2 us (86%)
  local copies, waits for them, and re-layouts  12.1 us (13%)
    pallas_call x1, Pallas kernels, on_device(): pl.pallas_call(kernel, out_shape=jax.ShapeDtypeStruct((R, D), BF16), in_s...  79.2 us
    unnamed x2, local copies, waits for them, and re-layouts  8.26 us

profile of v1, /device:TPU:16, one launch (start us, length us, event | category | flops | bytes accessed | tf_op | source)
XLA Modules:
  0.0 91.4 jit_solution(1700196800498567328)
XLA Ops:
  0.0 1.3 %broadcast_in_dim.22.offset_x = f32[1,640]{1,0:T(1,128)} reshape(f32[640]{0:T(1024)} %param.19) | data formatting | bytes 5120 | tf_op jit(solution)/shard_map/broadcast_in_dim | solution.py:511
  1.3 1.3 %broadcast_in_dim.27.norm_gain = f32[1,640]{1,0:T(1,128)} reshape(f32[640]{0:T(1024)} %param.24) | data formatting | bytes 5120 | tf_op jit(solution)/shard_map/broadcast_in_dim | solution.py:512
  2.6 1.3 %broadcast_in_dim.21.pre_gain = f32[1,2560]{1,0:T(1,128)} reshape(f32[2560]{0:T(1024)} %param.14) | data formatting | bytes 20480 | tf_op jit(solution)/shard_map/broadcast_in_dim | solution.py:511
  3.9 6.4 %copy.16 = bf16[2560,2,640]{2,0,1:T(8,128)(2,1)} copy(bf16[2560,2,640]{2,1,0:T(2,128)(2,1)} %param.15) | data formatting | bytes 13107200 | tf_op args[2]
  10.3 79.2 %shard_map.127 = bf16[96,2560]{1,0:T(8,128)(2,1)} custom-call(bf16[96,2560]{1,0:T(8,128)(2,1)} %tokens.1, f32[1,2560]{1,0:T(1,128)} %broadcast_in_dim.21.pre_gain, bf16[2,2560,640]{2,1,0:T(8,128)(2,1)} %bitcast.8, bf16[336,2560]{1,0:T(8,128)(2,1)} %bitcast.9, f32[4,640]{1,0:T(4,128)} %kernel_x.1, f32[4,256]{1,0:T(4,128)} %kernel_bc.1, ...), custom_call_target="tpu_custom_call" | custom-call | tf_op jit(solution)/shard_map/pallas_call | solution.py:501
  89.5 1.8 %copy.18 = bf16[96,2560]{1,0:T(8,128)(2,1)} copy(bf16[96,2560]{1,0:T(8,128)(2,1)} %shard_map.127) | data formatting | bytes 983040

commit v2 on v1

--- a/solution.py
+++ b/solution.py
@@ -50,7 +50,8 @@
 
 
 def silu(v):
-    return v / (1.0 + jnp.exp(-v))
+    half = 0.5 * v
+    return half + half * jnp.tanh(half)
 
 
 def remote(src, dst, send, recv, device):
@@ -60,14 +61,15 @@
 
 
 def kernel(
-    tokens, pre_gain, w_hbm, wo_hbm, kernel_x, kernel_bc, offset_x, offset_bc, dt_bias, a_log,
-    skip_gain, norm_gain, wout_hbm,
+    tokens_in, pre_gain_in, w_hbm, wo_hbm, kernel_x_in, kernel_bc_in, offset_x_in, offset_bc_in, dt_bias_in,
+    a_log_in, skip_gain_in, norm_gain_in, wout_hbm,
     out,
-    w, wo, wout, rows, xin, dtr, zs, xb, bmat, cmat, dts, cum, expand, ef, sl, sacc, pdr, pdacc,
+    tokens, pre_gain_v, kernel_x, kernel_bc, offset_x_v, offset_bc, dt_bias, a_log, skip_gain, norm_gain_v,
+    wraw, w, wo, wout, rows, xin, dtr, zs, xb, bmat, cmat, dts, cum, expand, ef, sl, pdr,
     yv, sb, drow, rz, rd, pz, pdz, tb, tdb, ty, tdy, cacc, pb, cr, gb, sqc, part, pr, ps, rl, rf,
-    sqs, sqr, small,
+    sqs, sqr, small, pre_gain, offset_x, norm_gain,
     ag_s, ag_r, halo_s, halo_r, zs_s, zs_r, zd_s, zd_r, y_s, y_r, yd_s, yd_r, bk_s, bk_r,
-    pp_s, pp_r, rl_s, rl_r, rf_s, rf_r, sq_s, sq_r, w_s,
+    pp_s, pp_r, rl_s, rl_r, rf_s, rf_r, sq_s, sq_r, w_s, in_s,
 ):
     s = lax.axis_index("seq")
     h = lax.axis_index("head")
@@ -81,14 +83,6 @@
     xo = (x + 2) % NX
     hr, hl, ho = xr * 2 + c, xl * 2 + c, xo * 2 + c
 
-    w_copies = [
-        pltpu.make_async_copy(w_hbm, w, w_s.at[0]),
-        pltpu.make_async_copy(wo_hbm, wo, w_s.at[1]),
-        pltpu.make_async_copy(wout_hbm, wout, w_s.at[2]),
-    ]
-    for cp in w_copies:
-        cp.start()
-
     barrier = pltpu.get_barrier_semaphore()
     for k in range(1, 8):
         pl.semaphore_signal(barrier, inc=1, device_id=(s, (h + k) % 8), device_id_type=MESH)
@@ -98,6 +92,26 @@
         pl.semaphore_signal(barrier, inc=1, device_id=(((y + k) % NY) * NZ + z, h), device_id_type=MESH)
     for k in (1, 31):
         pl.semaphore_signal(barrier, inc=1, device_id=((s + k) % 32, h), device_id_type=MESH)
+
+    pairs = (
+        (tokens_in, tokens), (pre_gain_in, pre_gain_v), (kernel_x_in, kernel_x), (kernel_bc_in, kernel_bc),
+        (offset_x_in, offset_x_v), (offset_bc_in, offset_bc), (dt_bias_in, dt_bias), (a_log_in, a_log),
+        (skip_gain_in, skip_gain), (norm_gain_in, norm_gain_v),
+    )
+    in_copies = [pltpu.make_async_copy(src, dst, in_s.at[i]) for i, (src, dst) in enumerate(pairs)]
+    w_copies = [
+        pltpu.make_async_copy(w_hbm, wraw, w_s.at[0]),
+        pltpu.make_async_copy(wo_hbm, wo, w_s.at[1]),
+        pltpu.make_async_copy(wout_hbm, wout, w_s.at[2]),
+    ]
+    for cp in in_copies + w_copies:
+        cp.start()
+    for cp in in_copies:
+        cp.wait()
+
+    for src, dst in ((pre_gain_v, pre_gain), (offset_x_v, offset_x), (norm_gain_v, norm_gain)):
+        for i in range(src.shape[0]):
+            dst[0:1, i * Q : (i + 1) * Q] = src[i : i + 1, :]
 
     for half in range(2):
         tk = tokens[half * HALF : (half + 1) * HALF, :].astype(F32)
@@ -129,21 +143,49 @@
     for cp in w_copies:
         cp.wait()
 
-    def project(chip, with_x, with_z):
+    pick_r = lax.broadcasted_iota(jnp.int32, (2 * Q, 2 * Q), 0)
+    pick_c = lax.broadcasted_iota(jnp.int32, (2 * Q, 2 * Q), 1)
+    pick_t = jnp.where(pick_r < Q, 2 * pick_r, 2 * (pick_r - Q) + 1)
+    pick = jnp.where(pick_c == pick_t, 1.0, 0.0).astype(BF16)
+    wflat = wraw.reshape(2 * D, DL)
+
+    def split_step(i, carry):
+        v = wflat[pl.ds(pl.multiple_of(i * 2 * Q, 2 * Q), 2 * Q), :]
+        r = dot(pick, v).astype(BF16)
+        w[0, pl.ds(pl.multiple_of(i * Q, Q), Q), :] = r[0:Q, :]
+        w[1, pl.ds(pl.multiple_of(i * Q, Q), Q), :] = r[Q : 2 * Q, :]
+        return carry
+
+    lax.fori_loop(0, D // Q, split_step, 0)
+
+    def put_rows(n, places):
+        xv = dot(n, w[1]).astype(BF16).astype(F32)
+        bv = dot_t(n, wo[0 : 2 * NS, :]).astype(BF16).astype(F32)
+        dv = dot_t(n, wo[2 * NS : 2 * NS + 80, :])
+        for at, lo, hi in places:
+            xin[pl.ds(pl.multiple_of(at + 8, 8), hi - lo), 0:DL] = xv[lo:hi, :]
+            xin[pl.ds(pl.multiple_of(at + 8, 8), hi - lo), DL : DL + 2 * NS] = bv[lo:hi, :]
+            dtr[pl.ds(pl.multiple_of(at, 8), hi - lo), 0:80] = dv[lo:hi, :]
+
+    def project_x(chip):
         n = rows[pl.ds(2 * chip, 2)].reshape(CH, D)
-        at = pl.multiple_of(chip * CH, CH)
-        if with_x:
-            xin[pl.ds(pl.multiple_of(at + 8, 8), CH), 0:DL] = dot(n, w[1]).astype(BF16).astype(F32)
-            xin[pl.ds(pl.multiple_of(at + 8, 8), CH), DL : DL + 2 * NS] = (
-                dot_t(n, wo[0 : 2 * NS, :]).astype(BF16).astype(F32)
-            )
-            dtr[pl.ds(at, CH), 0:80] = dot_t(n, wo[2 * NS : 2 * NS + 80, :])
-        if with_z:
-            zz = dot(n, w[0]).astype(BF16).astype(F32)
-            zs[pl.ds(at, CH), :] = silu(zz)
-
-    remote(rows.at[partner], rows.at[partner], ag_s.at[6], ag_r.at[6], (s, partner)).wait_recv()
-    project(x, True, True)
+        put_rows(n, [(chip * CH, 0, CH)])
+
+    def project_halves(chip_a, half_a, chip_b, half_b):
+        n = jnp.concatenate(
+            [rows[pl.ds(2 * chip_a, 2), half_a].reshape(R, D), rows[pl.ds(2 * chip_b, 2), half_b].reshape(R, D)],
+            axis=0,
+        )
+        places = []
+        for i, (chip, half) in enumerate(((chip_a, half_a), (chip_b, half_b))):
+            for core in range(2):
+                lo = i * R + core * HALF
+                places.append((chip * CH + core * R + half * HALF, lo, lo + HALF))
+        put_rows(n, places)
+
+    def project_z(chip):
+        n = rows[pl.ds(2 * chip, 2)].reshape(CH, D)
+        zs[pl.ds(pl.multiple_of(chip * CH, CH), CH), :] = silu(dot(n, w[0]).astype(BF16).astype(F32))
 
     def to_partner(origin, half, role):
         cp = ag(origin, half, 7 + role, partner)
@@ -153,67 +195,25 @@
     def partner_done(chip, half, role):
         ag(chip * 2 + 1 - c, half, 7 + role, partner).wait_recv()
 
-    ag(hl, 0, 0, hr).wait_recv()
-    cp = ag(hl, 0, 4, hr)
-    cp.start()
-    sends.append(cp)
-    ag(hr, 1, 3, hl).wait_recv()
-    cp = ag(hr, 1, 5, hl)
-    cp.start()
-    sends.append(cp)
-    to_partner(hl, 0, 0)
-    to_partner(hr, 1, 3)
-    ag(hl, 1, 1, hr).wait_recv()
-    to_partner(hl, 1, 1)
-    ag(hr, 0, 2, hl).wait_recv()
-    to_partner(hr, 0, 2)
-    partner_done(xl, 0, 0)
-    partner_done(xl, 1, 1)
-    project(xl, True, True)
-    partner_done(xr, 1, 3)
-    partner_done(xr, 0, 2)
-    project(xr, True, True)
-    ag(ho, 0, 4, hr).wait_recv()
-    to_partner(ho, 0, 4)
-    ag(ho, 1, 5, hl).wait_recv()
-    to_partner(ho, 1, 5)
-    partner_done(xo, 0, 4)
-    partner_done(xo, 1, 5)
-    project(xo, True, False)
-
-    halo = remote(xin.at[pl.ds(T, 8)], xin.at[pl.ds(0, 8)], halo_s, halo_r, ((s + 1) % 32, h))
-
-    @pl.when(s < 31)
-    def _():
-        halo.start()
+    def onward(origin, half, role, device):
+        cp = ag(origin, half, role, device)
+        cp.start()
+        sends.append(cp)
 
     lane = lax.broadcasted_iota(jnp.int32, (1, Q), 1)
     ri = lax.broadcasted_iota(jnp.int32, (Q, Q), 0)
     ci = lax.broadcasted_iota(jnp.int32, (Q, Q), 1)
     tri = jnp.where(ri >= ci, 1.0, 0.0).astype(BF16)
-    bias_row = small[0:1, :]
-    rate_row = -jnp.exp(small[1:2, :])
     shift = (Q - h * HEADS) % Q
-    total = jnp.zeros((1, Q), F32)
-    for q in range(NQ):
-        raw = pltpu.roll(dtr[q * Q : (q + 1) * Q, :], shift, 1) + bias_row
+
+    def step_sizes(q):
+        raw = pltpu.roll(dtr[pl.ds(pl.multiple_of(q * Q, Q), Q), :], shift, 1) + small[0:1, :]
         step = jnp.maximum(raw, 0.0) + jnp.log1p(jnp.exp(-jnp.abs(raw)))
         step = jnp.where(lane < HEADS, step, 0.0)
-        la = step * rate_row
+        la = step * -jnp.exp(small[1:2, :])
         dts[q] = step
         p3 = dot(tri, jnp.concatenate(split3(la), axis=1))
-        cq = p3[:, 0:Q] + p3[:, Q : 2 * Q] + p3[:, 2 * Q : 3 * Q]
-        cum[q] = cq
-        total = total + cq[Q - 1 : Q, :]
-    drow[...] = jnp.broadcast_to(jnp.exp(total), (8, Q))
-    rd[z] = drow[...]
-
-    def z_peer(k):
-        return (z + k) % NZ
-
-    for k in range(1, NZ):
-        zp = z_peer(k)
-        remote(drow, rd.at[z], zd_s.at[k], zd_r.at[z], (y * NZ + zp, h)).start()
+        cum[q] = p3[:, 0:Q] + p3[:, Q : 2 * Q] + p3[:, 2 * Q : 3 * Q]
 
     def conv_block(i):
         at = pl.multiple_of(i * 64, 64)
@@ -229,11 +229,89 @@
                 bmat[pl.ds(at, 64), :] = v[:, 0:NS]
                 cmat[pl.ds(at, 64), :] = v[:, NS : 2 * NS]
 
-    def conv_step(i, carry):
-        conv_block(i)
+    far = xo // 2
+    near = 1 - far
+    odd = xo % 2
+    late = 3 * far + odd
+    other = 3 * far + 2 - 2 * odd
+
+    def conv_early(i, carry):
+        chip = (x + 3 + i // 3) % NX
+        block = 3 * chip + i % 3
+        block = jnp.where(jnp.logical_or(block == 0, i == 0), block + 1, block)
+        conv_block(block)
         return carry
 
-    lax.fori_loop(1, T // 64, conv_step, 0)
+    ag(hl, 0, 0, hr).wait_recv()
+    onward(hl, 0, 4, hr)
+    ag(hr, 1, 3, hl).wait_recv()
+    onward(hr, 1, 5, hl)
+    to_partner(hl, 0, 0)
+    to_partner(hr, 1, 3)
+    remote(rows.at[partner], rows.at[partner], ag_s.at[6], ag_r.at[6], (s, partner)).wait_recv()
+    project_x(x)
+    partner_done(xl, 0, 0)
+    partner_done(xr, 1, 3)
+    project_halves(xl, 0, xr, 1)
+    ag(hl, 1, 1, hr).wait_recv()
+    to_partner(hl, 1, 1)
+    ag(hr, 0, 2, hl).wait_recv()
+    to_partner(hr, 0, 2)
+    lax.fori_loop(4, 6, conv_early, 0)
+    partner_done(xl, 1, 1)
+    partner_done(xr, 0, 2)
+    project_halves(xl, 1, xr, 0)
+    for q in (3 * near, 3 * near + 1, 3 * near + 2, other):
+        step_sizes(q)
+
+    lax.fori_loop(1, 4, conv_early, 0)
+    ag(ho, 0, 4, hr).wait_recv()
+    to_partner(ho, 0, 4)
+    ag(ho, 1, 5, hl).wait_recv()
+    to_partner(ho, 1, 5)
+    put_rows(rows[ho].reshape(R, D), [(ho * R, 0, R)])
+    lax.fori_loop(6, 9, conv_early, 0)
+    partner_done(xo, 0, 4)
+    partner_done(xo, 1, 5)
+    hop = 2 * xo + 1 - c
+    put_rows(rows[hop].reshape(R, D), [(hop * R, 0, R)])
+
+    halo = remote(xin.at[pl.ds(T, 8)], xin.at[pl.ds(0, 8)], halo_s, halo_r, ((s + 1) % 32, h))
+
+    @pl.when(s < 31)
+    def _():
+        halo.start()
+
+    step_sizes(late)
+    step_sizes(late + 1)
+    total = cum[0][Q - 1 : Q, :]
+    for q in range(1, NQ):
+        total = total + cum[q][Q - 1 : Q, :]
+    drow[...] = jnp.broadcast_to(jnp.exp(total), (8, Q))
+    rd[z] = drow[...]
+
+    def z_peer(k):
+        return (z + k) % NZ
+
+    for k in range(1, NZ):
+        zp = z_peer(k)
+        remote(drow, rd.at[z], zd_s.at[k], zd_r.at[z], (y * NZ + zp, h)).start()
+
+    conv_block(3 * xo + 1)
+    conv_block(3 * xo + 2)
+    conv_block(jnp.where(xo == 0, 3 * xl, 3 * xo))
+    conv_block(jnp.where(xl == 0, 3 * xo, 3 * xl))
+
+    def chunk_state(q):
+        cq = cum[q]
+        fac = jnp.exp(cq[Q - 1 : Q, :] - cq) * dts[q]
+        fx = dot(jnp.concatenate(split2(fac), axis=1), expand[...])
+        ef[q] = dot(jnp.concatenate(split2(jnp.exp(cq)), axis=1), expand[...])
+        xw = (xb[q * Q : (q + 1) * Q, :].astype(F32) * fx).astype(BF16)
+        sl[q] = t_dot(bmat[q * Q : (q + 1) * Q, :], xw)
+
+    for q in range(1, NQ):
+        chunk_state(q)
 
     @pl.when(s == 0)
     def _():
@@ -244,39 +322,30 @@
         halo.wait_recv()
 
     conv_block(0)
-
-    sacc[...] = jnp.zeros_like(sacc)
-    pdacc[...] = jnp.ones_like(pdacc)
-
-    def state_step(q, carry):
-        at = pl.multiple_of(q * Q, Q)
-        cq = cum[q]
-        fac = jnp.exp(cq[Q - 1 : Q, :] - cq) * dts[q]
-        fx = dot(jnp.concatenate(split2(fac), axis=1), expand[...])
-        ex = dot(jnp.concatenate(split2(jnp.exp(cq)), axis=1), expand[...])
-        ef[q] = ex
-        xw = (xb[pl.ds(at, Q), :].astype(F32) * fx).astype(BF16)
-        st = t_dot(bmat[pl.ds(at, Q), :], xw)
-        dec = ex[Q - 1 : Q, :]
-        prev = sacc[...]
-        sl[q] = prev
-        sacc[...] = prev * dec + st
-        pdr[q] = pdacc[...]
-        pdacc[...] = pdacc[...] * dec
-        return carry
-
-    lax.fori_loop(0, NQ, state_step, 0)
-    sb[...] = sacc[...].astype(BF16)
+    chunk_state(0)
+
+    for lo in range(0, DL, Q):
+        acc = jnp.zeros((NS, Q), F32)
+        pd = jnp.ones((1, Q), F32)
+        for q in range(NQ):
+            st = sl[q, :, lo : lo + Q]
+            dec = ef[q, Q - 1 : Q, lo : lo + Q]
+            sl[q, :, lo : lo + Q] = acc
+            pdr[q, 0:1, lo : lo + Q] = pd
+            acc = acc * dec + st
+            pd = pd * dec
+        sb[:, lo : lo + Q] = acc.astype(BF16)
     rz[z] = sb[pl.ds(pl.multiple_of(z * 16, 16), 16), :]
 
-    for k in range(1, NZ):
+    far_first = (4, 3, 5, 2, 6, 1, 7)
+    for k in far_first:
         zp = z_peer(k)
         remote(
             sb.at[pl.ds(pl.multiple_of(zp * 16, 16), 16)], rz.at[z], zs_s.at[k], zs_r.at[z],
             (y * NZ + zp, h),
         ).start()
 
-    project(xo, False, True)
+    project_z(xo)
     s3 = jnp.concatenate(split2(jnp.broadcast_to(small[2:3, :], (8, Q))), axis=1)
     skip_row = dot(s3, expand[...])[0:1, :]
     low = lax.broadcasted_iota(jnp.int32, (Q, Q), 1) < 64
@@ -326,6 +395,8 @@
             remote(tb, ty.at[y], y_s.at[k], y_r.at[y], dev).start()
             remote(tdb, tdy.at[y], yd_s.at[k], yd_r.at[y], dev).start()
 
+    project_z(xl)
+    project_z(x)
     cacc[...] = jnp.zeros_like(cacc)
     for k in range(NY - 1):
         @pl.when(k < y)
@@ -338,9 +409,10 @@
     for k in range(NZ):
         pb[k] = (pz[k] + pdz[k][0:1, :] * cacc[...]).astype(BF16)
     cr[z] = pb[z]
-    for k in range(1, NZ):
+    for k in far_first:
         zp = z_peer(k)
         remote(pb.at[zp], cr.at[z], bk_s.at[k], bk_r.at[z], (y * NZ + zp, h)).start()
+    project_z(xr)
     for k in range(1, NZ):
         zp = z_peer(k)
         remote(pb.at[zp], cr.at[zp], bk_s.at[k], bk_r.at[zp], (y * NZ + zp, h)).wait_recv()
@@ -354,17 +426,22 @@
         gb[pl.ds(at, Q), :] = (g * norm_gain[...]).astype(BF16)
         return carry
 
-    pair_sends = []
+    def pair_copy(d, lo, width, sem):
+        return remote(
+            part.at[2 * d + 1 - c, :, :, pl.ds(lo, width)], pr.at[d, :, :, pl.ds(lo, width)],
+            pp_s.at[sem], pp_r.at[sem], (s, partner),
+        )
+
+    def out_part(d, lo, width, sem):
+        n = gb[pl.ds(pl.multiple_of(d * CH, CH), CH), :]
+        for at in range(lo, lo + width, 256):
+            part[pl.ds(2 * d, 2), :, :, at : at + 256] = (
+                dot(n, wout[:, at : at + 256]).astype(BF16).reshape(2, 2, HALF, 256)
+            )
+        pair_copy(d, lo, width, sem).start()
 
     def out_chip(d):
-        n = gb[pl.ds(pl.multiple_of(d * CH, CH), CH), :]
-        for lo in range(0, D, 512):
-            part[pl.ds(2 * d, 2), :, :, lo : lo + 512] = (
-                dot(n, wout[:, lo : lo + 512]).astype(BF16).reshape(2, 2, HALF, 512)
-            )
-        cp = remote(part.at[2 * d + 1 - c], pr.at[d], pp_s.at[d], pp_r.at[d], (s, partner))
-        cp.start()
-        pair_sends.append(cp)
+        out_part(d, 0, D, d)
 
     def pair_sum(d, half):
         return part[2 * d + c, half].astype(F32) + pr[d, half].astype(F32)
@@ -372,21 +449,44 @@
     def pair_wait(d):
         remote(part.at[0], pr.at[d], pp_s.at[d], pp_r.at[d], (s, partner)).wait_recv()
 
-    first = xo // 2
     d1 = xo + 1 - 2 * (xo % 2)
     d2 = x + 1 - 2 * (x % 2)
-    lax.fori_loop(first * 3, first * 3 + 3, out_step, 0)
-    out_chip(xo)
-    out_chip(d1)
-    pair_wait(xo)
-    for half in range(2):
-        ps[0, half] = pair_sum(xo, half).astype(BF16)
-    relays = [
-        remote(ps.at[0, 0], rl.at[0], rl_s.at[0], rl_r.at[0], (s, hr)),
-        remote(ps.at[0, 1], rl.at[1], rl_s.at[1], rl_r.at[1], (s, hl)),
-    ]
-    for cp in relays:
-        cp.start()
+    out_step(late, 0)
+    out_step(late + 1, 0)
+    cols = D // 2
+
+    def relay_copy(half, i):
+        here = pl.ds(i * cols, cols)
+        return remote(
+            ps.at[0, half, :, here], rl.at[half, :, here], rl_s.at[half, i], rl_r.at[half, i],
+            (s, hl if half else hr),
+        )
+
+    def relay(i):
+        here = pl.ds(i * cols, cols)
+        pair_copy(xo, i * cols, cols, 4 + i).wait_recv()
+        for half in range(2):
+            ps[0, half, :, here] = (
+                part[2 * xo + c, half, :, here].astype(F32) + pr[xo, half, :, here].astype(F32)
+            ).astype(BF16)
+            relay_copy(half, i).start()
+
+    @pl.when(c == 0)
+    def _():
+        for i in range(2):
+            out_part(xo, i * cols, cols, 4 + i)
+            relay(i)
+        out_step(other, 0)
+        out_chip(d1)
+
+    @pl.when(c == 1)
+    def _():
+        for i in range(2):
+            out_part(xo, i * cols, cols, 4 + i)
+        out_step(other, 0)
+        out_chip(d1)
+        for i in range(2):
+            relay(i)
 
     def side_of(d):
         return jnp.where(d == xr, 0, 1)
@@ -409,13 +509,16 @@
 
     def send_relayed(slot, d):
         half = side_of(d)
-        remote(ps.at[0, 0], rl.at[half], rl_s.at[half], rl_r.at[half], (s, hr)).wait_recv()
+        for i in range(2):
+            here = pl.ds(i * cols, cols)
+            remote(
+                ps.at[0, 0, :, here], rl.at[half, :, here], rl_s.at[half, i], rl_r.at[half, i], (s, hr)
+            ).wait_recv()
         ps[slot, half] = (pair_sum(d, half) + rl[half].astype(F32)).astype(BF16)
         final_send(slot, d, half)
 
     send_direct(1, d1)
-    second = x // 2
-    lax.fori_loop(second * 3, second * 3 + 3, out_step, 0)
+    lax.fori_loop(near * 3, near * 3 + 3, out_step, 0)
     out_chip(d2)
     send_direct(2, d2)
     send_relayed(1, d1)
@@ -451,8 +554,14 @@
         ).astype(BF16)
 
     own_pair.wait_send()
-    for cp in sends + pair_sends + relays + finals + sq_sends:
+    for cp in sends + finals + sq_sends:
         cp.wait_send()
+    for i in range(2):
+        pair_copy(xo, i * cols, cols, 4 + i).wait_send()
+        for half in range(2):
+            relay_copy(half, i).wait_send()
+    for d in (d1, d2, x):
+        pair_copy(d, 0, D, d).wait_send()
 
     @pl.when(s < 31)
     def _():
@@ -476,41 +585,46 @@
     tokens, pre_gain, inner_proj, outer_proj, kernel_x, kernel_bc, offset_x, offset_bc, dt_bias, a_log,
     skip_gain, norm_gain, out_proj,
 ):
-    w = jnp.transpose(inner_proj, (1, 0, 2))
     vm = pl.BlockSpec(memory_space=pltpu.VMEM)
-    hbm = pl.BlockSpec(memory_space=pl.ANY)
+    hbm = pl.BlockSpec(memory_space=pltpu.HBM)
     dma = pltpu.SemaphoreType.DMA
     V = pltpu.VMEM
     scratch = [
-        V((2, D, DL), BF16), V((336, D), BF16), V((DL, D), BF16), V((8, 2, HALF, D), BF16),
+        V((R, D), BF16), V((D // Q, Q), F32), V((4, DL), F32), V((4, 2 * NS), F32), V((DL // Q, Q), F32),
+        V((1, 2 * NS), F32), V((1, HEADS), F32), V((1, HEADS), F32), V((1, HEADS), F32), V((DL // Q, Q), F32),
+        V((D, 2, DL), BF16), V((2, D, DL), BF16), V((336, D), BF16), V((DL, D), BF16), V((8, 2, HALF, D), BF16),
         V((T + 8, DL + 2 * NS), F32), V((T, Q), F32), V((T, DL), F32), V((T, DL), BF16),
         V((T, NS), BF16), V((T, NS), BF16), V((NQ, Q, Q), F32), V((NQ, Q, Q), F32),
-        V((2 * Q, DL), BF16), V((NQ, Q, DL), F32), V((NQ, NS, DL), F32), V((NS, DL), F32),
-        V((NQ, 8, DL), F32), V((8, DL), F32),
+        V((2 * Q, DL), BF16), V((NQ, Q, DL), F32), V((NQ, NS, DL), F32),
+        V((NQ, 8, DL), F32),
         V((T, DL), F32), V((NS, DL), BF16), V((8, Q), F32), V((NZ, 16, DL), BF16), V((NZ, 8, Q), F32),
         V((NZ, 16, DL), F32), V((NZ, 8, DL), F32), V((16, DL), BF16), V((8, DL), F32),
         V((NY, 16, DL), BF16), V((NY, 8, DL), F32), V((16, DL), F32), V((NZ, 16, DL), BF16),
         V((NZ, 16, DL), BF16), V((T, DL), BF16), V((T + 32, Q), F32), V((8, 2, HALF, D), BF16),
         V((NX, 2, HALF, D), BF16), V((3, 2, HALF, D), BF16), V((2, HALF, D), BF16), V((2, 2, HALF, D), BF16),
-        V((8, 8, Q), F32), V((8, 8, Q), F32), V((8, Q), F32),
+        V((8, 8, Q), F32), V((8, 8, Q), F32), V((8, Q), F32), V((1, D), F32), V((1, DL), F32),
+        V((1, DL), F32),
         dma((13,)), dma((13,)), dma, dma, dma((NZ,)), dma((NZ,)), dma((NZ,)), dma((NZ,)),
         dma((NY,)), dma((NY,)), dma((NY,)), dma((NY,)), dma((NZ,)), dma((NZ,)),
-        dma((NX,)), dma((NX,)), dma((2,)), dma((2,)), dma((2, 2)), dma((2, 2)), dma((8,)), dma((8,)),
-        dma((3,)),
+        dma((6,)), dma((6,)), dma((2, 2)), dma((2, 2)), dma((2, 2)), dma((2, 2)), dma((8,)), dma((8,)),
+        dma((3,)), dma((10,)),
     ]
+    args = (
+        tokens, pre_gain.reshape(D // Q, Q), inner_proj, outer_proj.T, kernel_x, kernel_bc,
+        offset_x.reshape(DL // Q, Q), offset_bc[None], dt_bias[None], a_log[None], skip_gain[None],
+        norm_gain.reshape(DL // Q, Q), out_proj,
+    )
+    args = [pltpu.with_memory_space_constraint(v, pltpu.HBM) for v in args]
     return pl.pallas_call(
         kernel,
         out_shape=jax.ShapeDtypeStruct((R, D), BF16),
-        in_specs=[vm, vm, hbm, hbm, vm, vm, vm, vm, vm, vm, vm, vm, hbm],
+        in_specs=[hbm] * 13,
         out_specs=vm,
         scratch_shapes=scratch,
         compiler_params=pltpu.CompilerParams(
-            collective_id=0, has_side_effects=True, vmem_limit_bytes=66_000_000
+            collective_id=0, has_side_effects=True, vmem_limit_bytes=56_000_000
         ),
-    )(
-        tokens, pre_gain[None], w, outer_proj.T, kernel_x, kernel_bc, offset_x[None], offset_bc[None],
-        dt_bias[None], a_log[None], skip_gain[None], norm_gain[None], out_proj,
-    )
+    )(*args)
 
 
 def solution(mesh):

time: 91.9 us -> 72.2 us (0.79)
  local copies, waits for them, and re-layouts: 12.1 us -> 0.78 us
  Pallas kernels: 79.2 us -> 70.6 us
    pallas_call x1, Pallas kernels: 79.2 us -> 70.6 us  [on_device(): pl.pallas_call(kernel, out_shape=jax.ShapeDtypeStruct((R, D), BF16), in_s...]
    unnamed x2 -> x1, local copies, waits for them, and re-layouts: 8.26 us -> 0.78 us
    broadcast_in_dim x3 -> x0, local copies, waits for them, and re-layouts: 3.87 us -> none  [the longest x1 1.31 us: on_device(): pre_gain[None]]
where the time goes in v2:
time: 72.2 us; the launch traced here: 71.4 us
  Pallas kernels  70.6 us (98%)
  local copies, waits for them, and re-layouts  0.78 us (1%)
    pallas_call x1, Pallas kernels, on_device(): pl.pallas_call(kernel, out_shape=jax.ShapeDtypeStruct((R, D), BF16), in_s...  70.6 us

profile of v2, /device:TPU:16, one launch (start us, length us, event | category | flops | bytes accessed | tf_op | source)
XLA Modules:
  0.0 71.4 jit_solution(5860017318412552247)
XLA Ops:
  0.0 70.6 %shard_map.127 = bf16[96,2560]{1,0:T(8,128)(2,1)S(1)} custom-call(bf16[96,2560]{1,0:T(8,128)(2,1)} %tokens_in.1, f32[20,128]{1,0:T(8,128)} %bitcast.9, bf16[2560,2,640]{2,1,0:T(2,128)(2,1)} %w_hbm.1, bf16[336,2560]{1,0:T(8,128)(2,1)} %bitcast.8, f32[4,640]{1,0:T(4,128)} %kernel_x_in.1, f32[4,256]{1,0:T(4,128)} %kernel_bc_in.1, f32[5,128]{1,0:T(8,128)} %bitcast.10, ...), custom_call_target="tpu_custom_call" | custom-call | tf_op jit(solution)/shard_map/pallas_call | solution.py:618
  70.6 0.8 %copy.15 = bf16[96,2560]{1,0:T(8,128)(2,1)} copy(bf16[96,2560]{1,0:T(8,128)(2,1)S(1)} %shard_map.127) | data formatting | bytes 983040

commit v3 on v2

--- a/solution.py
+++ b/solution.py
@@ -1,5 +1,3 @@
-import functools
-
 import jax
 import jax.numpy as jnp
 from jax import lax
@@ -65,9 +63,9 @@
     a_log_in, skip_gain_in, norm_gain_in, wout_hbm,
     out,
     tokens, pre_gain_v, kernel_x, kernel_bc, offset_x_v, offset_bc, dt_bias, a_log, skip_gain, norm_gain_v,
-    wraw, w, wo, wout, rows, xin, dtr, zs, xb, bmat, cmat, dts, cum, expand, ef, sl, pdr,
+    wraw, wz, wx, wo, wout, rows, xin, dtr, zs, xb, bmat, cmat, dts, cum, expand, ef, sl, pdr,
     yv, sb, drow, rz, rd, pz, pdz, tb, tdb, ty, tdy, cacc, pb, cr, gb, sqc, part, pr, ps, rl, rf,
-    sqs, sqr, small, pre_gain, offset_x, norm_gain,
+    sqs, sqr, small, pre_gain, offset_x, norm_gain, tot,
     ag_s, ag_r, halo_s, halo_r, zs_s, zs_r, zd_s, zd_r, y_s, y_r, yd_s, yd_r, bk_s, bk_r,
     pp_s, pp_r, rl_s, rl_r, rf_s, rf_r, sq_s, sq_r, w_s, in_s,
 ):
@@ -99,19 +97,31 @@
         (skip_gain_in, skip_gain), (norm_gain_in, norm_gain_v),
     )
     in_copies = [pltpu.make_async_copy(src, dst, in_s.at[i]) for i, (src, dst) in enumerate(pairs)]
+    quarter = D // 4
     w_copies = [
-        pltpu.make_async_copy(w_hbm, wraw, w_s.at[0]),
-        pltpu.make_async_copy(wo_hbm, wo, w_s.at[1]),
-        pltpu.make_async_copy(wout_hbm, wout, w_s.at[2]),
+        pltpu.make_async_copy(
+            w_hbm.at[pl.ds(i * quarter, quarter)], wraw.at[pl.ds(i * quarter, quarter)], w_s.at[i]
+        )
+        for i in range(4)
     ]
-    for cp in in_copies + w_copies:
+    late_copies = [
+        pltpu.make_async_copy(wo_hbm, wo.at[pl.ds(0, 336)], w_s.at[4]),
+        pltpu.make_async_copy(wout_hbm, wout, w_s.at[5]),
+    ]
+    for cp in in_copies[0:2]:
         cp.start()
-    for cp in in_copies:
+    for cp in in_copies[2:]:
+        cp.start()
+    for cp in in_copies[0:2]:
         cp.wait()
-
-    for src, dst in ((pre_gain_v, pre_gain), (offset_x_v, offset_x), (norm_gain_v, norm_gain)):
+    for cp in w_copies:
+        cp.start()
+
+    def as_row(src, dst):
         for i in range(src.shape[0]):
             dst[0:1, i * Q : (i + 1) * Q] = src[i : i + 1, :]
+
+    as_row(pre_gain_v, pre_gain)
 
     for half in range(2):
         tk = tokens[half * HALF : (half + 1) * HALF, :].astype(F32)
@@ -130,6 +140,13 @@
     own_pair.start()
     for cp in sends:
         cp.start()
+
+    for cp in late_copies:
+        cp.start()
+    for cp in in_copies[2:]:
+        cp.wait()
+    as_row(offset_x_v, offset_x)
+    as_row(norm_gain_v, norm_gain)
 
     li = lax.broadcasted_iota(jnp.int32, (2 * Q, DL), 0)
     lc = lax.broadcasted_iota(jnp.int32, (2 * Q, DL), 1)
@@ -139,10 +156,6 @@
     small[0:1, 0:HEADS] = dt_bias[...]
     small[1:2, 0:HEADS] = a_log[...]
     small[2:3, 0:HEADS] = skip_gain[...]
-    dtr[...] = jnp.zeros_like(dtr)
-    for cp in w_copies:
-        cp.wait()
-
     pick_r = lax.broadcasted_iota(jnp.int32, (2 * Q, 2 * Q), 0)
     pick_c = lax.broadcasted_iota(jnp.int32, (2 * Q, 2 * Q), 1)
     pick_t = jnp.where(pick_r < Q, 2 * pick_r, 2 * (pick_r - Q) + 1)
@@ -152,20 +165,27 @@
     def split_step(i, carry):
         v = wflat[pl.ds(pl.multiple_of(i * 2 * Q, 2 * Q), 2 * Q), :]
         r = dot(pick, v).astype(BF16)
-        w[0, pl.ds(pl.multiple_of(i * Q, Q), Q), :] = r[0:Q, :]
-        w[1, pl.ds(pl.multiple_of(i * Q, Q), Q), :] = r[Q : 2 * Q, :]
+        wz[pl.ds(pl.multiple_of(i * Q, Q), Q), :] = r[0:Q, :]
+        wx[pl.ds(pl.multiple_of(i * Q, Q), Q), 0:DL] = r[Q : 2 * Q, :]
         return carry
 
-    lax.fori_loop(0, D // Q, split_step, 0)
+    for i in range(4):
+        w_copies[i].wait()
+        lax.fori_loop(i * quarter // Q, (i + 1) * quarter // Q, split_step, 0)
+    for cp in late_copies:
+        cp.wait()
+
+    wo[336:384, :] = jnp.zeros((48, D), BF16)
+    same = jnp.where(pick_r == pick_c, 1.0, 0.0).astype(BF16)
+    for i in range(D // (2 * Q)):
+        at = slice(i * 2 * Q, (i + 1) * 2 * Q)
+        wx[at, DL:] = dot_t(same, wo[:, at]).astype(BF16)
 
     def put_rows(n, places):
-        xv = dot(n, w[1]).astype(BF16).astype(F32)
-        bv = dot_t(n, wo[0 : 2 * NS, :]).astype(BF16).astype(F32)
-        dv = dot_t(n, wo[2 * NS : 2 * NS + 80, :])
+        r = dot(n, wx[...])
         for at, lo, hi in places:
-            xin[pl.ds(pl.multiple_of(at + 8, 8), hi - lo), 0:DL] = xv[lo:hi, :]
-            xin[pl.ds(pl.multiple_of(at + 8, 8), hi - lo), DL : DL + 2 * NS] = bv[lo:hi, :]
-            dtr[pl.ds(pl.multiple_of(at, 8), hi - lo), 0:80] = dv[lo:hi, :]
+            xin[pl.ds(pl.multiple_of(at + 8, 8), hi - lo), :] = r[lo:hi, 0 : DL + 2 * NS].astype(BF16).astype(F32)
+            dtr[pl.ds(pl.multiple_of(at, 8), hi - lo), :] = r[lo:hi, DL + 2 * NS :]
 
     def project_x(chip):
         n = rows[pl.ds(2 * chip, 2)].reshape(CH, D)
@@ -185,7 +205,7 @@
 
     def project_z(chip):
         n = rows[pl.ds(2 * chip, 2)].reshape(CH, D)
-        zs[pl.ds(pl.multiple_of(chip * CH, CH), CH), :] = silu(dot(n, w[0]).astype(BF16).astype(F32))
+        zs[pl.ds(pl.multiple_of(chip * CH, CH), CH), :] = silu(dot(n, wz[...]).astype(BF16).astype(F32))
 
     def to_partner(origin, half, role):
         cp = ag(origin, half, 7 + role, partner)
@@ -217,17 +237,25 @@
 
     def conv_block(i):
         at = pl.multiple_of(i * 64, 64)
-        for lo, hi, kern, off in ((0, DL, kernel_x, offset_x), (DL, DL + 2 * NS, kernel_bc, offset_bc)):
-            u = jnp.broadcast_to(off[...], (64, hi - lo))
-            v = xin[pl.ds(at, 72), lo:hi]
-            for k in range(4):
-                u = u + kern[k : k + 1, :] * v[5 + k : 69 + k, :]
-            v = silu(u).astype(BF16)
-            if lo == 0:
-                xb[pl.ds(at, 64), :] = v
+        for j in range((DL + 2 * NS) // Q):
+            kern, off, lo = (kernel_x, offset_x, j * Q) if j < 5 else (kernel_bc, offset_bc, (j - 5) * Q)
+            v = xin[pl.ds(at, 72), j * Q : (j + 1) * Q]
+            u = kern[0:1, lo : lo + Q] * v
+            for k in range(1, 4):
+                u = pltpu.roll(u, 1, 0) + kern[k : k + 1, lo : lo + Q] * v
+            v = silu(u[8:72, :] + off[:, lo : lo + Q]).astype(BF16)
+            if j < 5:
+                xb[pl.ds(at, 64), lo : lo + Q] = v
             else:
-                bmat[pl.ds(at, 64), :] = v[:, 0:NS]
-                cmat[pl.ds(at, 64), :] = v[:, NS : 2 * NS]
+                (bmat, cmat)[j - 5][pl.ds(at, 64), :] = v
+
+    def chunk_state(q):
+        at = pl.multiple_of(q * Q, Q)
+        cq = cum[q]
+        fac = jnp.exp(cq[Q - 1 : Q, :] - cq) * dts[q]
+        fx = dot(jnp.concatenate(split2(fac), axis=1), expand[...])
+        xw = (xb[pl.ds(at, Q), :].astype(F32) * fx).astype(BF16)
+        sl[q] = t_dot(bmat[pl.ds(at, Q), :], xw)
 
     far = xo // 2
     near = 1 - far
@@ -242,13 +270,13 @@
         conv_block(block)
         return carry
 
+    remote(rows.at[partner], rows.at[partner], ag_s.at[6], ag_r.at[6], (s, partner)).wait_recv()
     ag(hl, 0, 0, hr).wait_recv()
     onward(hl, 0, 4, hr)
     ag(hr, 1, 3, hl).wait_recv()
     onward(hr, 1, 5, hl)
     to_partner(hl, 0, 0)
     to_partner(hr, 1, 3)
-    remote(rows.at[partner], rows.at[partner], ag_s.at[6], ag_r.at[6], (s, partner)).wait_recv()
     project_x(x)
     partner_done(xl, 0, 0)
     partner_done(xr, 1, 3)
@@ -257,24 +285,53 @@
     to_partner(hl, 1, 1)
     ag(hr, 0, 2, hl).wait_recv()
     to_partner(hr, 0, 2)
+
+    @pl.when(c == 0)
+    def _():
+        partner_done(xl, 1, 1)
+        partner_done(xr, 0, 2)
+
+    def put_seconds(core):
+        n = jnp.concatenate([rows[2 * xl + core, 1], rows[2 * xr + core, 0]], axis=0)
+        put_rows(
+            n,
+            [(xl * CH + core * R + HALF, 0, HALF), (xr * CH + core * R, HALF, R)],
+        )
+
+    put_seconds(1)
     lax.fori_loop(4, 6, conv_early, 0)
-    partner_done(xl, 1, 1)
-    partner_done(xr, 0, 2)
-    project_halves(xl, 1, xr, 0)
+
+    @pl.when(c == 1)
+    def _():
+        partner_done(xl, 1, 1)
+        partner_done(xr, 0, 2)
+
+    put_seconds(0)
+
+    def opposite_in():
+        ag(ho, 0, 4, hr).wait_recv()
+        ag(ho, 0, 11, partner).start()
+        ag(ho, 1, 5, hl).wait_recv()
+        ag(ho, 1, 12, partner).start()
+
+    @pl.when(c == 1)
+    def _():
+        opposite_in()
+
     for q in (3 * near, 3 * near + 1, 3 * near + 2, other):
         step_sizes(q)
-
     lax.fori_loop(1, 4, conv_early, 0)
-    ag(ho, 0, 4, hr).wait_recv()
-    to_partner(ho, 0, 4)
-    ag(ho, 1, 5, hl).wait_recv()
-    to_partner(ho, 1, 5)
-    put_rows(rows[ho].reshape(R, D), [(ho * R, 0, R)])
+
+    @pl.when(c == 0)
+    def _():
+        opposite_in()
+
     lax.fori_loop(6, 9, conv_early, 0)
+    chunk_state(3 * near + 1)
+    chunk_state(3 * near + 2)
     partner_done(xo, 0, 4)
     partner_done(xo, 1, 5)
-    hop = 2 * xo + 1 - c
-    put_rows(rows[hop].reshape(R, D), [(hop * R, 0, R)])
+    project_x(xo)
 
     halo = remote(xin.at[pl.ds(T, 8)], xin.at[pl.ds(0, 8)], halo_s, halo_r, ((s + 1) % 32, h))
 
@@ -302,16 +359,9 @@
     conv_block(jnp.where(xo == 0, 3 * xl, 3 * xo))
     conv_block(jnp.where(xl == 0, 3 * xo, 3 * xl))
 
-    def chunk_state(q):
-        cq = cum[q]
-        fac = jnp.exp(cq[Q - 1 : Q, :] - cq) * dts[q]
-        fx = dot(jnp.concatenate(split2(fac), axis=1), expand[...])
-        ef[q] = dot(jnp.concatenate(split2(jnp.exp(cq)), axis=1), expand[...])
-        xw = (xb[q * Q : (q + 1) * Q, :].astype(F32) * fx).astype(BF16)
-        sl[q] = t_dot(bmat[q * Q : (q + 1) * Q, :], xw)
-
-    for q in range(1, NQ):
-        chunk_state(q)
+    rest = jnp.where(near == 0, 3, 1)
+    for k in range(3):
+        chunk_state(rest + k)
 
     @pl.when(s == 0)
     def _():
@@ -324,12 +374,14 @@
     conv_block(0)
     chunk_state(0)
 
+    ends = jnp.concatenate([cum[q][Q - 1 : Q, :] for q in range(NQ)] + [jnp.zeros((2, Q), F32)], axis=0)
+    decs = dot(jnp.concatenate(split2(jnp.exp(ends)), axis=1), expand[...])
     for lo in range(0, DL, Q):
         acc = jnp.zeros((NS, Q), F32)
         pd = jnp.ones((1, Q), F32)
         for q in range(NQ):
             st = sl[q, :, lo : lo + Q]
-            dec = ef[q, Q - 1 : Q, lo : lo + Q]
+            dec = decs[q : q + 1, lo : lo + Q]
             sl[q, :, lo : lo + Q] = acc
             pdr[q, 0:1, lo : lo + Q] = pd
             acc = acc * dec + st
@@ -353,6 +405,7 @@
     def intra_step(q, carry):
         at = pl.multiple_of(q * Q, Q)
         cq = cum[q]
+        ef[q] = dot(jnp.concatenate(split2(jnp.exp(cq)), axis=1), expand[...])
         cqt = jnp.transpose(cq)
         dtt = jnp.transpose(dts[q])
         cb = dot_t(cmat[pl.ds(at, Q), :], bmat[pl.ds(at, Q), :])
@@ -435,8 +488,9 @@
     def out_part(d, lo, width, sem):
         n = gb[pl.ds(pl.multiple_of(d * CH, CH), CH), :]
         for at in range(lo, lo + width, 256):
-            part[pl.ds(2 * d, 2), :, :, at : at + 256] = (
-                dot(n, wout[:, at : at + 256]).astype(BF16).reshape(2, 2, HALF, 256)
+            end = min(at + 256, lo + width)
+            part[pl.ds(2 * d, 2), :, :, at:end] = (
+                dot(n, wout[:, at:end]).astype(BF16).reshape(2, 2, HALF, end - at)
             )
         pair_copy(d, lo, width, sem).start()
 
@@ -453,18 +507,19 @@
     d2 = x + 1 - 2 * (x % 2)
     out_step(late, 0)
     out_step(late + 1, 0)
-    cols = D // 2
+    cuts = ((0, 512), (512, 896), (1408, 1152))
+    pieces = len(cuts)
 
     def relay_copy(half, i):
-        here = pl.ds(i * cols, cols)
+        here = pl.ds(*cuts[i])
         return remote(
             ps.at[0, half, :, here], rl.at[half, :, here], rl_s.at[half, i], rl_r.at[half, i],
             (s, hl if half else hr),
         )
 
     def relay(i):
-        here = pl.ds(i * cols, cols)
-        pair_copy(xo, i * cols, cols, 4 + i).wait_recv()
+        here = pl.ds(*cuts[i])
+        pair_copy(xo, *cuts[i], 4 + i).wait_recv()
         for half in range(2):
             ps[0, half, :, here] = (
                 part[2 * xo + c, half, :, here].astype(F32) + pr[xo, half, :, here].astype(F32)
@@ -473,20 +528,26 @@
 
     @pl.when(c == 0)
     def _():
-        for i in range(2):
-            out_part(xo, i * cols, cols, 4 + i)
-            relay(i)
+        for i in range(pieces):
+            out_part(xo, *cuts[i], 4 + i)
+            if i > 0:
+                relay(i - 1)
+        relay(pieces - 1)
         out_step(other, 0)
         out_chip(d1)
 
     @pl.when(c == 1)
     def _():
-        for i in range(2):
-            out_part(xo, i * cols, cols, 4 + i)
+        for i in range(pieces):
+            out_part(xo, *cuts[i], 4 + i)
+        relay(0)
         out_step(other, 0)
+        relay(1)
         out_chip(d1)
-        for i in range(2):
-            relay(i)
+        relay(2)
+
+    lax.fori_loop(near * 3, near * 3 + 3, out_step, 0)
+    out_chip(d2)
 
     def side_of(d):
         return jnp.where(d == xr, 0, 1)
@@ -509,8 +570,8 @@
 
     def send_relayed(slot, d):
         half = side_of(d)
-        for i in range(2):
-            here = pl.ds(i * cols, cols)
+        for i in range(pieces):
+            here = pl.ds(*cuts[i])
             remote(
                 ps.at[0, 0, :, here], rl.at[half, :, here], rl_s.at[half, i], rl_r.at[half, i], (s, hr)
             ).wait_recv()
@@ -518,13 +579,6 @@
         final_send(slot, d, half)
 
     send_direct(1, d1)
-    lax.fori_loop(near * 3, near * 3 + 3, out_step, 0)
-    out_chip(d2)
-    send_direct(2, d2)
-    send_relayed(1, d1)
-    send_relayed(2, d2)
-    out_chip(x)
-
     sq_sends = []
     for k in range(8):
         col = sqc[pl.ds(pl.multiple_of(((h + k) % 8) * R, 32), Q), :]
@@ -535,7 +589,21 @@
             cp = remote(sqs.at[(h + k) % 8], sqr.at[h], sq_s.at[k], sq_r.at[h], (s, (h + k) % 8))
             cp.start()
             sq_sends.append(cp)
+    send_direct(2, d2)
+    send_relayed(1, d1)
+    send_relayed(2, d2)
+    out_chip(x)
+
     pair_wait(x)
+
+    def final_wait(side, half):
+        remote(
+            ps.at[1, half], rf.at[side, half], rf_s.at[side, half], rf_r.at[side, half], (s, hl)
+        ).wait_recv()
+
+    for half in range(2):
+        final_wait(1 - half, half)
+        tot[half] = pair_sum(x, half) + rf[1 - half, half].astype(F32)
     for k in range(1, 8):
         hk = (h + k) % 8
         remote(sqs.at[0], sqr.at[hk], sq_s.at[k], sq_r.at[hk], (s, hk)).wait_recv()
@@ -543,21 +611,18 @@
     inv_row = lax.rsqrt(squares / (DL * 8) + NORM_FLOOR)
     inv_col = jnp.transpose(jnp.broadcast_to(inv_row, (Q, Q)))
     for half in range(2):
-        for side in range(2):
-            remote(
-                ps.at[1, half], rf.at[side, half], rf_s.at[side, half], rf_r.at[side, half], (s, hl)
-            ).wait_recv()
-    for half in range(2):
-        tot = pair_sum(x, half) + rf[0, half].astype(F32) + rf[1, half].astype(F32)
+        final_wait(half, half)
         out[half * HALF : (half + 1) * HALF, :] = (
-            tot * inv_col[half * HALF : (half + 1) * HALF, 0:1]
+            (tot[half] + rf[half, half].astype(F32)) * inv_col[half * HALF : (half + 1) * HALF, 0:1]
         ).astype(BF16)
 
     own_pair.wait_send()
+    ag(ho, 0, 11, partner).wait_send()
+    ag(ho, 1, 12, partner).wait_send()
     for cp in sends + finals + sq_sends:
         cp.wait_send()
-    for i in range(2):
-        pair_copy(xo, i * cols, cols, 4 + i).wait_send()
+    for i in range(pieces):
+        pair_copy(xo, *cuts[i], 4 + i).wait_send()
         for half in range(2):
             relay_copy(half, i).wait_send()
     for d in (d1, d2, x):
@@ -592,7 +657,7 @@
     scratch = [
         V((R, D), BF16), V((D // Q, Q), F32), V((4, DL), F32), V((4, 2 * NS), F32), V((DL // Q, Q), F32),
         V((1, 2 * NS), F32), V((1, HEADS), F32), V((1, HEADS), F32), V((1, HEADS), F32), V((DL // Q, Q), F32),
-        V((D, 2, DL), BF16), V((2, D, DL), BF16), V((336, D), BF16), V((DL, D), BF16), V((8, 2, HALF, D), BF16),
+        V((D, 2, DL), BF16), V((D, DL), BF16), V((D, 1024), BF16), V((384, D), BF16), V((DL, D), BF16), V((8, 2, HALF, D), BF16),
         V((T + 8, DL + 2 * NS), F32), V((T, Q), F32), V((T, DL), F32), V((T, DL), BF16),
         V((T, NS), BF16), V((T, NS), BF16), V((NQ, Q, Q), F32), V((NQ, Q, Q), F32),
         V((2 * Q, DL), BF16), V((NQ, Q, DL), F32), V((NQ, NS, DL), F32),
@@ -603,11 +668,11 @@
         V((NZ, 16, DL), BF16), V((T, DL), BF16), V((T + 32, Q), F32), V((8, 2, HALF, D), BF16),
         V((NX, 2, HALF, D), BF16), V((3, 2, HALF, D), BF16), V((2, HALF, D), BF16), V((2, 2, HALF, D), BF16),
         V((8, 8, Q), F32), V((8, 8, Q), F32), V((8, Q), F32), V((1, D), F32), V((1, DL), F32),
-        V((1, DL), F32),
+        V((1, DL), F32), V((2, HALF, D), F32),
         dma((13,)), dma((13,)), dma, dma, dma((NZ,)), dma((NZ,)), dma((NZ,)), dma((NZ,)),
         dma((NY,)), dma((NY,)), dma((NY,)), dma((NY,)), dma((NZ,)), dma((NZ,)),
-        dma((6,)), dma((6,)), dma((2, 2)), dma((2, 2)), dma((2, 2)), dma((2, 2)), dma((8,)), dma((8,)),
-        dma((3,)), dma((10,)),
+        dma((7,)), dma((7,)), dma((2, 3)), dma((2, 3)), dma((2, 2)), dma((2, 2)), dma((8,)), dma((8,)),
+        dma((6,)), dma((10,)),
     ]
     args = (
         tokens, pre_gain.reshape(D // Q, Q), inner_proj, outer_proj.T, kernel_x, kernel_bc,
@@ -622,7 +687,7 @@
         out_specs=vm,
         scratch_shapes=scratch,
         compiler_params=pltpu.CompilerParams(
-            collective_id=0, has_side_effects=True, vmem_limit_bytes=56_000_000
+            collective_id=0, has_side_effects=True, vmem_limit_bytes=55_000_000
         ),
     )(*args)
 

time: 72.2 us -> 70.2 us (0.972)
  Pallas kernels: 70.6 us -> 68.6 us
    pallas_call x1, Pallas kernels: 70.6 us -> 68.6 us  [on_device(): pl.pallas_call(kernel, out_shape=jax.ShapeDtypeStruct((R, D), BF16), in_s...]
where the time goes in v3:
time: 70.2 us; the launch traced here: 69.4 us
  Pallas kernels  68.6 us (98%)
  local copies, waits for them, and re-layouts  0.78 us (1%)
    pallas_call x1, Pallas kernels, on_device(): pl.pallas_call(kernel, out_shape=jax.ShapeDtypeStruct((R, D), BF16), in_s...  68.6 us

profile of v3, /device:TPU:16, one launch (start us, length us, event | category | flops | bytes accessed | tf_op | source)
XLA Modules:
  0.0 69.4 jit_solution(3745648634479830827)
XLA Ops:
  0.0 68.6 %shard_map.127 = bf16[96,2560]{1,0:T(8,128)(2,1)S(1)} custom-call(bf16[96,2560]{1,0:T(8,128)(2,1)} %tokens_in.1, f32[20,128]{1,0:T(8,128)} %bitcast.9, bf16[2560,2,640]{2,1,0:T(2,128)(2,1)} %w_hbm.1, bf16[336,2560]{1,0:T(8,128)(2,1)} %bitcast.8, f32[4,640]{1,0:T(4,128)} %kernel_x_in.1, f32[4,256]{1,0:T(4,128)} %kernel_bc_in.1, f32[5,128]{1,0:T(8,128)} %bitcast.10, ...), custom_call_target="tpu_custom_call" | custom-call | tf_op jit(solution)/shard_map/pallas_call | solution.py:683
  68.6 0.8 %copy.15 = bf16[96,2560]{1,0:T(8,128)(2,1)} copy(bf16[96,2560]{1,0:T(8,128)(2,1)S(1)} %shard_map.127) | data formatting | bytes 983040

commit v4 on v3

--- a/solution.py
+++ b/solution.py
@@ -63,7 +63,7 @@
     a_log_in, skip_gain_in, norm_gain_in, wout_hbm,
     out,
     tokens, pre_gain_v, kernel_x, kernel_bc, offset_x_v, offset_bc, dt_bias, a_log, skip_gain, norm_gain_v,
-    wraw, wz, wx, wo, wout, rows, xin, dtr, zs, xb, bmat, cmat, dts, cum, expand, ef, sl, pdr,
+    wraw, wz, wx, wo, wout, rows, xin, dtr, zs, xb, bmat, cmat, dts, cum, expand, ef, sl, sacc, pdr,
     yv, sb, drow, rz, rd, pz, pdz, tb, tdb, ty, tdy, cacc, pb, cr, gb, sqc, part, pr, ps, rl, rf,
     sqs, sqr, small, pre_gain, offset_x, norm_gain, tot,
     ag_s, ag_r, halo_s, halo_r, zs_s, zs_r, zd_s, zd_r, y_s, y_r, yd_s, yd_r, bk_s, bk_r,
@@ -81,11 +81,16 @@
     xo = (x + 2) % NX
     hr, hl, ho = xr * 2 + c, xl * 2 + c, xo * 2 + c
 
+    def await_bytes(like, sem):
+        pltpu.make_async_copy(like, like, sem).wait()
+
     barrier = pltpu.get_barrier_semaphore()
     for k in range(1, 8):
         pl.semaphore_signal(barrier, inc=1, device_id=(s, (h + k) % 8), device_id_type=MESH)
     for k in range(1, NZ):
         pl.semaphore_signal(barrier, inc=1, device_id=(y * NZ + (z + k) % NZ, h), device_id_type=MESH)
+    for k in range(1, NZ):
+        pl.semaphore_signal(barrier, inc=1, device_id=(y * NZ + (z + k) % NZ, partner), device_id_type=MESH)
     for k in range(1, NY):
         pl.semaphore_signal(barrier, inc=1, device_id=(((y + k) % NY) * NZ + z, h), device_id_type=MESH)
     for k in (1, 31):
@@ -128,14 +133,14 @@
         inv = lax.rsqrt(jnp.mean(tk * tk, axis=1, keepdims=True) + NORM_FLOOR)
         rows[h, half] = (tk * inv * pre_gain[...]).astype(BF16)
 
-    pl.semaphore_wait(barrier, 19)
+    pl.semaphore_wait(barrier, 26)
 
     def ag(origin, half, role, device):
         return remote(
-            rows.at[origin, half], rows.at[origin, half], ag_s.at[role], ag_r.at[role], (s, device)
-        )
-
-    own_pair = remote(rows.at[h], rows.at[h], ag_s.at[6], ag_r.at[6], (s, partner))
+            rows.at[origin, half], rows.at[origin, half], ag_s, ag_r.at[role], (s, device)
+        )
+
+    own_pair = remote(rows.at[h], rows.at[h], ag_s, ag_r.at[6], (s, partner))
     sends = [ag(h, 0, 0, hr), ag(h, 1, 3, hl), ag(h, 1, 1, hr), ag(h, 0, 2, hl)]
     own_pair.start()
     for cp in sends:
@@ -270,7 +275,7 @@
         conv_block(block)
         return carry
 
-    remote(rows.at[partner], rows.at[partner], ag_s.at[6], ag_r.at[6], (s, partner)).wait_recv()
+    remote(rows.at[partner], rows.at[partner], ag_s, ag_r.at[6], (s, partner)).wait_recv()
     ag(hl, 0, 0, hr).wait_recv()
     onward(hl, 0, 4, hr)
     ag(hr, 1, 3, hl).wait_recv()
@@ -345,14 +350,44 @@
     for q in range(1, NQ):
         total = total + cum[q][Q - 1 : Q, :]
     drow[...] = jnp.broadcast_to(jnp.exp(total), (8, Q))
-    rd[z] = drow[...]
+
+    owner = 2 * x + 1
+    far_first = (4, 3, 5, 2, 6, 1, 7)
 
     def z_peer(k):
         return (z + k) % NZ
 
+    def rate_copy(k):
+        return remote(
+            drow, rd.at[c, z], zd_s, zd_r.at[c], (y * NZ + z_peer(k), owner)
+        )
+
+    def state_copy(k):
+        at = pl.multiple_of(z_peer(k) * 16, 16)
+        return remote(
+            sb.at[pl.ds(at, 16)], rz.at[c, z], zs_s, zs_r.at[c], (y * NZ + z_peer(k), owner)
+        )
+
+    def sum_copy(k):
+        return remote(tb, ty.at[y], y_s.at[k], y_r.at[y], ((y + k) % NY * NZ + z, h))
+
+    def sum_rate_copy(k):
+        return remote(tdb, tdy.at[y], yd_s.at[k], yd_r.at[y], ((y + k) % NY * NZ + z, h))
+
+    def back_copy(g, k):
+        zp = z_peer(k)
+        return remote(pb.at[g, zp], cr.at[z], bk_s, bk_r, (y * NZ + zp, 2 * x + g))
+
     for k in range(1, NZ):
-        zp = z_peer(k)
-        remote(drow, rd.at[z], zd_s.at[k], zd_r.at[z], (y * NZ + zp, h)).start()
+        rate_copy(k).start()
+
+    @pl.when(c == 0)
+    def _():
+        rate_copy(0).start()
+
+    @pl.when(c == 1)
+    def _():
+        rd[1, z] = drow[...]
 
     conv_block(3 * xo + 1)
     conv_block(3 * xo + 2)
@@ -363,6 +398,14 @@
     for k in range(3):
         chunk_state(rest + k)
 
+    ends = jnp.concatenate([cum[q][Q - 1 : Q, :] for q in range(NQ)] + [jnp.zeros((2, Q), F32)], axis=0)
+    decs = dot(jnp.concatenate(split2(jnp.exp(ends)), axis=1), expand[...])
+    for lo in range(0, DL, Q):
+        acc = sl[1, :, lo : lo + Q]
+        for q in range(2, NQ):
+            acc = acc * decs[q : q + 1, lo : lo + Q] + sl[q, :, lo : lo + Q]
+        sacc[:, lo : lo + Q] = acc
+
     @pl.when(s == 0)
     def _():
         xin[0:8, :] = jnp.zeros((8, DL + 2 * NS), F32)
@@ -373,9 +416,22 @@
 
     conv_block(0)
     chunk_state(0)
-
-    ends = jnp.concatenate([cum[q][Q - 1 : Q, :] for q in range(NQ)] + [jnp.zeros((2, Q), F32)], axis=0)
-    decs = dot(jnp.concatenate(split2(jnp.exp(ends)), axis=1), expand[...])
+    later = decs[1:2, :]
+    for q in range(2, NQ):
+        later = later * decs[q : q + 1, :]
+    sb[...] = (sacc[...] + later * sl[0]).astype(BF16)
+
+    for k in far_first:
+        state_copy(k).start()
+
+    @pl.when(c == 0)
+    def _():
+        state_copy(0).start()
+
+    @pl.when(c == 1)
+    def _():
+        rz[1, z] = sb[pl.ds(pl.multiple_of(z * 16, 16), 16), :]
+
     for lo in range(0, DL, Q):
         acc = jnp.zeros((NS, Q), F32)
         pd = jnp.ones((1, Q), F32)
@@ -386,16 +442,6 @@
             pdr[q, 0:1, lo : lo + Q] = pd
             acc = acc * dec + st
             pd = pd * dec
-        sb[:, lo : lo + Q] = acc.astype(BF16)
-    rz[z] = sb[pl.ds(pl.multiple_of(z * 16, 16), 16), :]
-
-    far_first = (4, 3, 5, 2, 6, 1, 7)
-    for k in far_first:
-        zp = z_peer(k)
-        remote(
-            sb.at[pl.ds(pl.multiple_of(zp * 16, 16), 16)], rz.at[z], zs_s.at[k], zs_r.at[z],
-            (y * NZ + zp, h),
-        ).start()
 
     project_z(xo)
     s3 = jnp.concatenate(split2(jnp.broadcast_to(small[2:3, :], (8, Q))), axis=1)
@@ -425,50 +471,64 @@
 
     lax.fori_loop(0, NQ, intra_step, 0)
 
-    for k in range(1, NZ):
-        zp = z_peer(k)
-        remote(drow, rd.at[zp], zd_s.at[k], zd_r.at[zp], (y * NZ + zp, h)).wait_recv()
-        remote(sb.at[pl.ds(0, 16)], rz.at[zp], zs_s.at[k], zs_r.at[zp], (y * NZ + zp, h)).wait_recv()
-    dz = jnp.concatenate([rd[k][0:1, :] for k in range(NZ)], axis=0)
-    dx = dot(jnp.concatenate(split2(dz), axis=1), expand[...])
-    acc = jnp.zeros((16, DL), F32)
-    pd = jnp.ones((1, DL), F32)
-    for k in range(NZ):
-        pz[k] = acc
-        pdz[k] = jnp.broadcast_to(pd, (8, DL))
-        acc = acc * dx[k : k + 1, :] + rz[k].astype(F32)
-        pd = pd * dx[k : k + 1, :]
-    tb[...] = acc.astype(BF16)
-    tdb[...] = jnp.broadcast_to(pd, (8, DL))
-
-    for k in range(1, NY):
-        @pl.when(y + k < NY)
-        def _(k=k):
-            dev = ((y + k) % NY * NZ + z, h)
-            remote(tb, ty.at[y], y_s.at[k], y_r.at[y], dev).start()
-            remote(tdb, tdy.at[y], yd_s.at[k], yd_r.at[y], dev).start()
+    @pl.when(c == 1)
+    def _():
+        for g in (1, 0):
+            if g == 1:
+                await_bytes(dtr.at[pl.ds(0, 56)], zd_r.at[1])
+                await_bytes(xb.at[pl.ds(0, 112)], zs_r.at[1])
+            else:
+                await_bytes(rd.at[0], zd_r.at[0])
+                await_bytes(rz.at[0], zs_r.at[0])
+            dz = jnp.concatenate([rd[g, k][0:1, :] for k in range(NZ)], axis=0)
+            dx = dot(jnp.concatenate(split2(dz), axis=1), expand[...])
+            acc = jnp.zeros((16, DL), F32)
+            pd = jnp.ones((1, DL), F32)
+            for k in range(NZ):
+                pz[g, k] = acc
+                pdz[g, k] = jnp.broadcast_to(pd, (8, DL))
+                acc = acc * dx[k : k + 1, :] + rz[g, k].astype(F32)
+                pd = pd * dx[k : k + 1, :]
+            tb[g] = acc.astype(BF16)
+            tdb[g] = jnp.broadcast_to(pd, (8, DL))
+        for k in range(1, NY):
+            @pl.when(y + k < NY)
+            def _(k=k):
+                sum_copy(k).start()
+                sum_rate_copy(k).start()
 
     project_z(xl)
     project_z(x)
-    cacc[...] = jnp.zeros_like(cacc)
-    for k in range(NY - 1):
-        @pl.when(k < y)
-        def _(k=k):
-            dev = (k * NZ + z, h)
-            remote(tb, ty.at[k], y_s.at[1], y_r.at[k], dev).wait_recv()
-            remote(tdb, tdy.at[k], yd_s.at[1], yd_r.at[k], dev).wait_recv()
-            cacc[...] = cacc[...] * tdy[k][0:1, :] + ty[k].astype(F32)
-
-    for k in range(NZ):
-        pb[k] = (pz[k] + pdz[k][0:1, :] * cacc[...]).astype(BF16)
-    cr[z] = pb[z]
-    for k in far_first:
-        zp = z_peer(k)
-        remote(pb.at[zp], cr.at[z], bk_s.at[k], bk_r.at[z], (y * NZ + zp, h)).start()
+
+    @pl.when(c == 1)
+    def _():
+        cacc[...] = jnp.zeros_like(cacc)
+        for k in range(NY - 1):
+            @pl.when(k < y)
+            def _(k=k):
+                dev = (k * NZ + z, h)
+                remote(tb, ty.at[k], y_s.at[1], y_r.at[k], dev).wait_recv()
+                remote(tdb, tdy.at[k], yd_s.at[1], yd_r.at[k], dev).wait_recv()
+                for g in range(2):
+                    cacc[g] = cacc[g] * tdy[k, g][0:1, :] + ty[k, g].astype(F32)
+        for g in range(2):
+            for k in range(NZ):
+                pb[g, k] = (pz[g, k] + pdz[g, k][0:1, :] * cacc[g]).astype(BF16)
+        for k in far_first:
+            for g in range(2):
+                back_copy(g, k).start()
+        back_copy(0, 0).start()
+        cr[z] = pb[1, z]
+
     project_z(xr)
-    for k in range(1, NZ):
-        zp = z_peer(k)
-        remote(pb.at[zp], cr.at[zp], bk_s.at[k], bk_r.at[zp], (y * NZ + zp, h)).wait_recv()
+
+    @pl.when(c == 1)
+    def _():
+        await_bytes(xb.at[pl.ds(0, 112)], bk_r)
+
+    @pl.when(c == 0)
+    def _():
+        await_bytes(cr, bk_r)
 
     def out_step(q, carry):
         at = pl.multiple_of(q * Q, Q)
@@ -482,7 +542,7 @@
     def pair_copy(d, lo, width, sem):
         return remote(
             part.at[2 * d + 1 - c, :, :, pl.ds(lo, width)], pr.at[d, :, :, pl.ds(lo, width)],
-            pp_s.at[sem], pp_r.at[sem], (s, partner),
+            pp_s, pp_r.at[sem], (s, partner),
         )
 
     def out_part(d, lo, width, sem):
@@ -501,7 +561,7 @@
         return part[2 * d + c, half].astype(F32) + pr[d, half].astype(F32)
 
     def pair_wait(d):
-        remote(part.at[0], pr.at[d], pp_s.at[d], pp_r.at[d], (s, partner)).wait_recv()
+        remote(part.at[0], pr.at[d], pp_s, pp_r.at[d], (s, partner)).wait_recv()
 
     d1 = xo + 1 - 2 * (xo % 2)
     d2 = x + 1 - 2 * (x % 2)
@@ -513,7 +573,7 @@
     def relay_copy(half, i):
         here = pl.ds(*cuts[i])
         return remote(
-            ps.at[0, half, :, here], rl.at[half, :, here], rl_s.at[half, i], rl_r.at[half, i],
+            ps.at[0, half, :, here], rl.at[half, :, here], rl_s, rl_r.at[half, i],
             (s, hl if half else hr),
         )
 
@@ -557,7 +617,7 @@
     def final_send(slot, d, half):
         side = side_of(d)
         cp = remote(
-            ps.at[slot, half], rf.at[side, half], rf_s.at[side, half], rf_r.at[side, half], (s, 2 * d + c)
+            ps.at[slot, half], rf.at[side, half], rf_s, rf_r.at[side, half], (s, 2 * d + c)
         )
         cp.start()
         finals.append(cp)
@@ -573,7 +633,7 @@
         for i in range(pieces):
             here = pl.ds(*cuts[i])
             remote(
-                ps.at[0, 0, :, here], rl.at[half, :, here], rl_s.at[half, i], rl_r.at[half, i], (s, hr)
+                ps.at[0, 0, :, here], rl.at[half, :, here], rl_s, rl_r.at[half, i], (s, hr)
             ).wait_recv()
         ps[slot, half] = (pair_sum(d, half) + rl[half].astype(F32)).astype(BF16)
         final_send(slot, d, half)
@@ -586,7 +646,7 @@
         if k == 0:
             sqr[h] = sqs[h]
         else:
-            cp = remote(sqs.at[(h + k) % 8], sqr.at[h], sq_s.at[k], sq_r.at[h], (s, (h + k) % 8))
+            cp = remote(sqs.at[(h + k) % 8], sqr.at[h], sq_s, sq_r, (s, (h + k) % 8))
             cp.start()
             sq_sends.append(cp)
     send_direct(2, d2)
@@ -598,15 +658,13 @@
 
     def final_wait(side, half):
         remote(
-            ps.at[1, half], rf.at[side, half], rf_s.at[side, half], rf_r.at[side, half], (s, hl)
+            ps.at[1, half], rf.at[side, half], rf_s, rf_r.at[side, half], (s, hl)
         ).wait_recv()
 
     for half in range(2):
         final_wait(1 - half, half)
         tot[half] = pair_sum(x, half) + rf[1 - half, half].astype(F32)
-    for k in range(1, 8):
-        hk = (h + k) % 8
-        remote(sqs.at[0], sqr.at[hk], sq_s.at[k], sq_r.at[hk], (s, hk)).wait_recv()
+    await_bytes(dtr.at[pl.ds(0, 56)], sq_r)
     squares = jnp.sum(sqr[...], axis=0)[0:1, :]
     inv_row = lax.rsqrt(squares / (DL * 8) + NORM_FLOOR)
     inv_col = jnp.transpose(jnp.broadcast_to(inv_row, (Q, Q)))
@@ -616,34 +674,31 @@
             (tot[half] + rf[half, half].astype(F32)) * inv_col[half * HALF : (half + 1) * HALF, 0:1]
         ).astype(BF16)
 
-    own_pair.wait_send()
-    ag(ho, 0, 11, partner).wait_send()
-    ag(ho, 1, 12, partner).wait_send()
-    for cp in sends + finals + sq_sends:
-        cp.wait_send()
-    for i in range(pieces):
-        pair_copy(xo, *cuts[i], 4 + i).wait_send()
-        for half in range(2):
-            relay_copy(half, i).wait_send()
-    for d in (d1, d2, x):
-        pair_copy(d, 0, D, d).wait_send()
+    await_bytes(rows.at[pl.ds(0, 7)], ag_s)
+    await_bytes(part.at[pl.ds(0, 4)], pp_s)
+    await_bytes(part.at[0], rl_s)
+    await_bytes(part.at[pl.ds(0, 2)], rf_s)
+    await_bytes(dtr.at[pl.ds(0, 56)], sq_s)
 
     @pl.when(s < 31)
     def _():
         halo.wait_send()
 
-    for k in range(1, NZ):
-        zp = z_peer(k)
-        dev = (y * NZ + zp, h)
-        remote(drow, rd.at[z], zd_s.at[k], zd_r.at[z], dev).wait_send()
-        remote(sb.at[pl.ds(0, 16)], rz.at[z], zs_s.at[k], zs_r.at[z], dev).wait_send()
-        remote(pb.at[zp], cr.at[z], bk_s.at[k], bk_r.at[z], dev).wait_send()
-    for k in range(1, NY):
-        @pl.when(y + k < NY)
-        def _(k=k):
-            dev = ((y + k) % NY * NZ + z, h)
-            remote(tb, ty.at[y], y_s.at[k], y_r.at[y], dev).wait_send()
-            remote(tdb, tdy.at[y], yd_s.at[k], yd_r.at[y], dev).wait_send()
+    @pl.when(c == 0)
+    def _():
+        await_bytes(rd.at[0], zd_s)
+        await_bytes(rz.at[0], zs_s)
+
+    @pl.when(c == 1)
+    def _():
+        await_bytes(dtr.at[pl.ds(0, 56)], zd_s)
+        await_bytes(xb.at[pl.ds(0, 112)], zs_s)
+        await_bytes(xb.at[pl.ds(0, 240)], bk_s)
+        for k in range(1, NY):
+            @pl.when(y + k < NY)
+            def _(k=k):
+                sum_copy(k).wait_send()
+                sum_rate_copy(k).wait_send()
 
 
 def on_device(
@@ -660,18 +715,18 @@
         V((D, 2, DL), BF16), V((D, DL), BF16), V((D, 1024), BF16), V((384, D), BF16), V((DL, D), BF16), V((8, 2, HALF, D), BF16),
         V((T + 8, DL + 2 * NS), F32), V((T, Q), F32), V((T, DL), F32), V((T, DL), BF16),
         V((T, NS), BF16), V((T, NS), BF16), V((NQ, Q, Q), F32), V((NQ, Q, Q), F32),
-        V((2 * Q, DL), BF16), V((NQ, Q, DL), F32), V((NQ, NS, DL), F32),
+        V((2 * Q, DL), BF16), V((NQ, Q, DL), F32), V((NQ, NS, DL), F32), V((NS, DL), F32),
         V((NQ, 8, DL), F32),
-        V((T, DL), F32), V((NS, DL), BF16), V((8, Q), F32), V((NZ, 16, DL), BF16), V((NZ, 8, Q), F32),
-        V((NZ, 16, DL), F32), V((NZ, 8, DL), F32), V((16, DL), BF16), V((8, DL), F32),
-        V((NY, 16, DL), BF16), V((NY, 8, DL), F32), V((16, DL), F32), V((NZ, 16, DL), BF16),
+        V((T, DL), F32), V((NS, DL), BF16), V((8, Q), F32), V((2, NZ, 16, DL), BF16), V((2, NZ, 8, Q), F32),
+        V((2, NZ, 16, DL), F32), V((2, NZ, 8, DL), F32), V((2, 16, DL), BF16), V((2, 8, DL), F32),
+        V((NY, 2, 16, DL), BF16), V((NY, 2, 8, DL), F32), V((2, 16, DL), F32), V((2, NZ, 16, DL), BF16),
         V((NZ, 16, DL), BF16), V((T, DL), BF16), V((T + 32, Q), F32), V((8, 2, HALF, D), BF16),
         V((NX, 2, HALF, D), BF16), V((3, 2, HALF, D), BF16), V((2, HALF, D), BF16), V((2, 2, HALF, D), BF16),
         V((8, 8, Q), F32), V((8, 8, Q), F32), V((8, Q), F32), V((1, D), F32), V((1, DL), F32),
         V((1, DL), F32), V((2, HALF, D), F32),
-        dma((13,)), dma((13,)), dma, dma, dma((NZ,)), dma((NZ,)), dma((NZ,)), dma((NZ,)),
-        dma((NY,)), dma((NY,)), dma((NY,)), dma((NY,)), dma((NZ,)), dma((NZ,)),
-        dma((7,)), dma((7,)), dma((2, 3)), dma((2, 3)), dma((2, 2)), dma((2, 2)), dma((8,)), dma((8,)),
+        dma, dma((13,)), dma, dma, dma, dma((2,)), dma, dma((2,)),
+        dma((NY,)), dma((NY,)), dma((NY,)), dma((NY,)), dma, dma,
+        dma, dma((7,)), dma, dma((2, 3)), dma, dma((2, 2)), dma, dma,
         dma((6,)), dma((10,)),
     ]
     args = (

time: 70.2 us -> 69.6 us (level); the launches traced: 69.4 us -> 69.5 us
  no operation moved by 1% of the time
where the time goes in v4:
time: 69.6 us; the launch traced here: 69.5 us
  Pallas kernels  68.7 us (99%)
  local copies, waits for them, and re-layouts  0.78 us (1%)
    pallas_call x1, Pallas kernels, on_device(): pl.pallas_call(kernel, out_shape=jax.ShapeDtypeStruct((R, D), BF16), in_s...  68.7 us

profile of v4, /device:TPU:16, one launch (start us, length us, event | category | flops | bytes accessed | tf_op | source)
XLA Modules:
  0.0 69.5 jit_solution(10833301606401742046)
XLA Ops:
  0.0 68.7 %shard_map.127 = bf16[96,2560]{1,0:T(8,128)(2,1)S(1)} custom-call(bf16[96,2560]{1,0:T(8,128)(2,1)} %tokens_in.1, f32[20,128]{1,0:T(8,128)} %bitcast.9, bf16[2560,2,640]{2,1,0:T(2,128)(2,1)} %w_hbm.1, bf16[336,2560]{1,0:T(8,128)(2,1)} %bitcast.8, f32[4,640]{1,0:T(4,128)} %kernel_x_in.1, f32[4,256]{1,0:T(4,128)} %kernel_bc_in.1, f32[5,128]{1,0:T(8,128)} %bitcast.10, ...), custom_call_target="tpu_custom_call" | custom-call | tf_op jit(solution)/shard_map/pallas_call | solution.py:738
  68.8 0.8 %copy.15 = bf16[96,2560]{1,0:T(8,128)(2,1)} copy(bf16[96,2560]{1,0:T(8,128)(2,1)S(1)} %shard_map.127) | data formatting | bytes 983040

commit v5 on v4

--- a/solution.py
+++ b/solution.py
@@ -64,7 +64,7 @@
     out,
     tokens, pre_gain_v, kernel_x, kernel_bc, offset_x_v, offset_bc, dt_bias, a_log, skip_gain, norm_gain_v,
     wraw, wz, wx, wo, wout, rows, xin, dtr, zs, xb, bmat, cmat, dts, cum, expand, ef, sl, sacc, pdr,
-    yv, sb, drow, rz, rd, pz, pdz, tb, tdb, ty, tdy, cacc, pb, cr, gb, sqc, part, pr, ps, rl, rf,
+    yv, sb, drow, rz, rd, dxs, pz, pdz, tb, tdb, ty, tdy, cacc, pb, cr, gb, sqc, part, pr, ps, rl, rf,
     sqs, sqr, small, pre_gain, offset_x, norm_gain, tot,
     ag_s, ag_r, halo_s, halo_r, zs_s, zs_r, zd_s, zd_r, y_s, y_r, yd_s, yd_r, bk_s, bk_r,
     pp_s, pp_r, rl_s, rl_r, rf_s, rf_r, sq_s, sq_r, w_s, in_s,
@@ -326,12 +326,13 @@
     for q in (3 * near, 3 * near + 1, 3 * near + 2, other):
         step_sizes(q)
     lax.fori_loop(1, 4, conv_early, 0)
+    lax.fori_loop(6, 8, conv_early, 0)
 
     @pl.when(c == 0)
     def _():
         opposite_in()
 
-    lax.fori_loop(6, 9, conv_early, 0)
+    lax.fori_loop(8, 9, conv_early, 0)
     chunk_state(3 * near + 1)
     chunk_state(3 * near + 2)
     partner_done(xo, 0, 4)
@@ -369,10 +370,10 @@
         )
 
     def sum_copy(k):
-        return remote(tb, ty.at[y], y_s.at[k], y_r.at[y], ((y + k) % NY * NZ + z, h))
+        return remote(tb, ty.at[y], y_s.at[k - 1], y_r.at[y], ((y + k) % NY * NZ + z, h))
 
     def sum_rate_copy(k):
-        return remote(tdb, tdy.at[y], yd_s.at[k], yd_r.at[y], ((y + k) % NY * NZ + z, h))
+        return remote(tdb, tdy.at[y], yd_s.at[k - 1], yd_r.at[y], ((y + k) % NY * NZ + z, h))
 
     def back_copy(g, k):
         zp = z_peer(k)
@@ -476,26 +477,36 @@
         for g in (1, 0):
             if g == 1:
                 await_bytes(dtr.at[pl.ds(0, 56)], zd_r.at[1])
-                await_bytes(xb.at[pl.ds(0, 112)], zs_r.at[1])
             else:
                 await_bytes(rd.at[0], zd_r.at[0])
-                await_bytes(rz.at[0], zs_r.at[0])
             dz = jnp.concatenate([rd[g, k][0:1, :] for k in range(NZ)], axis=0)
             dx = dot(jnp.concatenate(split2(dz), axis=1), expand[...])
-            acc = jnp.zeros((16, DL), F32)
+            dxs[g] = dx
             pd = jnp.ones((1, DL), F32)
             for k in range(NZ):
-                pz[g, k] = acc
                 pdz[g, k] = jnp.broadcast_to(pd, (8, DL))
-                acc = acc * dx[k : k + 1, :] + rz[g, k].astype(F32)
                 pd = pd * dx[k : k + 1, :]
-            tb[g] = acc.astype(BF16)
             tdb[g] = jnp.broadcast_to(pd, (8, DL))
         for k in range(1, NY):
             @pl.when(y + k < NY)
             def _(k=k):
+                sum_rate_copy(k).start()
+
+        for g in (1, 0):
+            if g == 1:
+                await_bytes(xb.at[pl.ds(0, 112)], zs_r.at[1])
+            else:
+                await_bytes(rz.at[0], zs_r.at[0])
+            dx = dxs[g]
+            acc = jnp.zeros((16, DL), F32)
+            for k in range(NZ):
+                pz[g, k] = acc
+                acc = acc * dx[k : k + 1, :] + rz[g, k].astype(F32)
+            tb[g] = acc.astype(BF16)
+        for k in (2, 1, 3):
+            @pl.when(y + k < NY)
+            def _(k=k):
                 sum_copy(k).start()
-                sum_rate_copy(k).start()
 
     project_z(xl)
     project_z(x)
@@ -507,8 +518,8 @@
             @pl.when(k < y)
             def _(k=k):
                 dev = (k * NZ + z, h)
-                remote(tb, ty.at[k], y_s.at[1], y_r.at[k], dev).wait_recv()
-                remote(tdb, tdy.at[k], yd_s.at[1], yd_r.at[k], dev).wait_recv()
+                remote(tb, ty.at[k], y_s.at[0], y_r.at[k], dev).wait_recv()
+                remote(tdb, tdy.at[k], yd_s.at[0], yd_r.at[k], dev).wait_recv()
                 for g in range(2):
                     cacc[g] = cacc[g] * tdy[k, g][0:1, :] + ty[k, g].astype(F32)
         for g in range(2):
@@ -717,7 +728,7 @@
         V((T, NS), BF16), V((T, NS), BF16), V((NQ, Q, Q), F32), V((NQ, Q, Q), F32),
         V((2 * Q, DL), BF16), V((NQ, Q, DL), F32), V((NQ, NS, DL), F32), V((NS, DL), F32),
         V((NQ, 8, DL), F32),
-        V((T, DL), F32), V((NS, DL), BF16), V((8, Q), F32), V((2, NZ, 16, DL), BF16), V((2, NZ, 8, Q), F32),
+        V((T, DL), F32), V((NS, DL), BF16), V((8, Q), F32), V((2, NZ, 16, DL), BF16), V((2, NZ, 8, Q), F32), V((2, NZ, DL), F32),
         V((2, NZ, 16, DL), F32), V((2, NZ, 8, DL), F32), V((2, 16, DL), BF16), V((2, 8, DL), F32),
         V((NY, 2, 16, DL), BF16), V((NY, 2, 8, DL), F32), V((2, 16, DL), F32), V((2, NZ, 16, DL), BF16),
         V((NZ, 16, DL), BF16), V((T, DL), BF16), V((T + 32, Q), F32), V((8, 2, HALF, D), BF16),
@@ -725,7 +736,7 @@
         V((8, 8, Q), F32), V((8, 8, Q), F32), V((8, Q), F32), V((1, D), F32), V((1, DL), F32),
         V((1, DL), F32), V((2, HALF, D), F32),
         dma, dma((13,)), dma, dma, dma, dma((2,)), dma, dma((2,)),
-        dma((NY,)), dma((NY,)), dma((NY,)), dma((NY,)), dma, dma,
+        dma((NY - 1,)), dma((NY - 1,)), dma((NY - 1,)), dma((NY - 1,)), dma, dma,
         dma, dma((7,)), dma, dma((2, 3)), dma, dma((2, 2)), dma, dma,
         dma((6,)), dma((10,)),
     ]

time: 69.6 us -> 69 us (level); the launches traced: 69.5 us -> 67.8 us
  Pallas kernels: 68.7 us -> 67 us
    pallas_call x1, Pallas kernels: 68.7 us -> 67 us  [on_device(): pl.pallas_call(kernel, out_shape=jax.ShapeDtypeStruct((R, D), BF16), in_s...]
where the time goes in v5:
time: 69 us; the launch traced here: 67.8 us
  Pallas kernels  67 us (97%)
  local copies, waits for them, and re-layouts  0.78 us (1%)
    pallas_call x1, Pallas kernels, on_device(): pl.pallas_call(kernel, out_shape=jax.ShapeDtypeStruct((R, D), BF16), in_s...  67 us

profile of v5, /device:TPU:16, one launch (start us, length us, event | category | flops | bytes accessed | tf_op | source)
XLA Modules:
  0.0 67.8 jit_solution(14164441271778112888)
XLA Ops:
  0.0 67.0 %shard_map.127 = bf16[96,2560]{1,0:T(8,128)(2,1)S(1)} custom-call(bf16[96,2560]{1,0:T(8,128)(2,1)} %tokens_in.1, f32[20,128]{1,0:T(8,128)} %bitcast.9, bf16[2560,2,640]{2,1,0:T(2,128)(2,1)} %w_hbm.1, bf16[336,2560]{1,0:T(8,128)(2,1)} %bitcast.8, f32[4,640]{1,0:T(4,128)} %kernel_x_in.1, f32[4,256]{1,0:T(4,128)} %kernel_bc_in.1, f32[5,128]{1,0:T(8,128)} %bitcast.10, ...), custom_call_target="tpu_custom_call" | custom-call | tf_op jit(solution)/shard_map/pallas_call | solution.py:749
  67.0 0.8 %copy.15 = bf16[96,2560]{1,0:T(8,128)(2,1)} copy(bf16[96,2560]{1,0:T(8,128)(2,1)S(1)} %shard_map.127) | data formatting | bytes 983040

commit v6 on v5

--- a/solution.py
+++ b/solution.py
@@ -492,6 +492,10 @@
             def _(k=k):
                 sum_rate_copy(k).start()
 
+    project_z(xl)
+
+    @pl.when(c == 1)
+    def _():
         for g in (1, 0):
             if g == 1:
                 await_bytes(xb.at[pl.ds(0, 112)], zs_r.at[1])
@@ -508,8 +512,6 @@
             def _(k=k):
                 sum_copy(k).start()
 
-    project_z(xl)
-    project_z(x)
 
     @pl.when(c == 1)
     def _():
@@ -531,6 +533,7 @@
         back_copy(0, 0).start()
         cr[z] = pb[1, z]
 
+    project_z(x)
     project_z(xr)
 
     @pl.when(c == 1)

time: 69 us -> 68.7 us (level)
  no operation moved by 1% of the time
where the time goes in v6:
time: 68.7 us; the launch traced here: 68 us
  Pallas kernels  67.2 us (98%)
  local copies, waits for them, and re-layouts  0.78 us (1%)
    pallas_call x1, Pallas kernels, on_device(): pl.pallas_call(kernel, out_shape=jax.ShapeDtypeStruct((R, D), BF16), in_s...  67.2 us

profile of v6, /device:TPU:16, one launch (start us, length us, event | category | flops | bytes accessed | tf_op | source)
XLA Modules:
  0.0 68.0 jit_solution(9532442772159838559)
XLA Ops:
  0.0 67.2 %shard_map.127 = bf16[96,2560]{1,0:T(8,128)(2,1)S(1)} custom-call(bf16[96,2560]{1,0:T(8,128)(2,1)} %tokens_in.1, f32[20,128]{1,0:T(8,128)} %bitcast.9, bf16[2560,2,640]{2,1,0:T(2,128)(2,1)} %w_hbm.1, bf16[336,2560]{1,0:T(8,128)(2,1)} %bitcast.8, f32[4,640]{1,0:T(4,128)} %kernel_x_in.1, f32[4,256]{1,0:T(4,128)} %kernel_bc_in.1, f32[5,128]{1,0:T(8,128)} %bitcast.10, ...), custom_call_target="tpu_custom_call" | custom-call | tf_op jit(solution)/shard_map/pallas_call | solution.py:752
  67.2 0.8 %copy.15 = bf16[96,2560]{1,0:T(8,128)(2,1)} copy(bf16[96,2560]{1,0:T(8,128)(2,1)S(1)} %shard_map.127) | data formatting | bytes 983040

commit v7 on v6

--- a/solution.py
+++ b/solution.py
@@ -313,6 +313,13 @@
 
     put_seconds(0)
 
+    halo = remote(xin.at[pl.ds(T, 8)], xin.at[pl.ds(0, 8)], halo_s, halo_r, ((s + 1) % 32, h))
+
+    @pl.when(jnp.logical_and(s < 31, xo != 3))
+    def _():
+        halo.start()
+
+
     def opposite_in():
         ag(ho, 0, 4, hr).wait_recv()
         ag(ho, 0, 11, partner).start()
@@ -339,9 +346,7 @@
     partner_done(xo, 1, 5)
     project_x(xo)
 
-    halo = remote(xin.at[pl.ds(T, 8)], xin.at[pl.ds(0, 8)], halo_s, halo_r, ((s + 1) % 32, h))
-
-    @pl.when(s < 31)
+    @pl.when(jnp.logical_and(s < 31, xo == 3))
     def _():
         halo.start()
 

time: 68.7 us -> 67.8 us (0.987)
  Pallas kernels: 67.2 us -> 66.2 us
    pallas_call x1, Pallas kernels: 67.2 us -> 66.2 us  [on_device(): pl.pallas_call(kernel, out_shape=jax.ShapeDtypeStruct((R, D), BF16), in_s...]
where the time goes in v7:
time: 67.8 us; the launch traced here: 67 us
  Pallas kernels  66.2 us (98%)
  local copies, waits for them, and re-layouts  0.78 us (1%)
    pallas_call x1, Pallas kernels, on_device(): pl.pallas_call(kernel, out_shape=jax.ShapeDtypeStruct((R, D), BF16), in_s...  66.2 us

profile of v7, /device:TPU:16, one launch (start us, length us, event | category | flops | bytes accessed | tf_op | source)
XLA Modules:
  0.0 67.0 jit_solution(8922920409147008984)
XLA Ops:
  0.0 66.2 %shard_map.127 = bf16[96,2560]{1,0:T(8,128)(2,1)S(1)} custom-call(bf16[96,2560]{1,0:T(8,128)(2,1)} %tokens_in.1, f32[20,128]{1,0:T(8,128)} %bitcast.9, bf16[2560,2,640]{2,1,0:T(2,128)(2,1)} %w_hbm.1, bf16[336,2560]{1,0:T(8,128)(2,1)} %bitcast.8, f32[4,640]{1,0:T(4,128)} %kernel_x_in.1, f32[4,256]{1,0:T(4,128)} %kernel_bc_in.1, f32[5,128]{1,0:T(8,128)} %bitcast.10, ...), custom_call_target="tpu_custom_call" | custom-call | tf_op jit(solution)/shard_map/pallas_call | solution.py:757
  66.3 0.8 %copy.15 = bf16[96,2560]{1,0:T(8,128)(2,1)} copy(bf16[96,2560]{1,0:T(8,128)(2,1)S(1)} %shard_map.127) | data formatting | bytes 983040
